TPU v7x, 32 devices: a 4x4x1 block of a 4x4x8 slice. The times are simulated.
32 devices in a mesh: dp: 1 (over z), ep: 32 (over y, x, core).
Axes of the slice: x: 4, y: 4, z: 1, core: 2. Of those that a mesh axis runs over, the one named last changes fastest.
The devices are a block of a 4x4x8 slice.
Arguments:
- x_in: bfloat16 [96, 512, 2048], P(('dp', 'ep'))
- pad_mask: int32 [96, 512], P(('dp', 'ep'))
- rel_bias: float32 [16, 512, 512], replicated
- expert_idx: int32 [2, 96, 512], P(None, ('dp', 'ep'))
- norm_scale: float32 [2, 2, 2048], replicated
- w_query: bfloat16 [2, 2048, 2048], replicated
- w_key: bfloat16 [2, 2048, 2048], replicated
- w_value: bfloat16 [2, 2048, 2048], replicated
- w_attn_out: bfloat16 [2, 2048, 2048], replicated
- w_router: float32 [2, 2048, 64], replicated
- w_in: bfloat16 [2, 64, 2048, 1024], P(None, 'ep')
- w_out: bfloat16 [2, 64, 1024, 2048], P(None, 'ep')
Outputs:
- output: bfloat16 [96, 512, 2048], P(('dp', 'ep'))
All inputs are finite; a program needn't handle non-finite values.
Results may differ from a plain program's by a relative error of at most 0.019653.
Values are sent between devices in bfloat16 or wider.
A program may use at most 768 MiB of HBM per device.

v0:
```python
import jax
import jax.numpy as jnp
from jax import lax
from jax.sharding import PartitionSpec as P, NamedSharding

NORM_EPS = 1e-6
NEG_BIG = -1e9
CAP_FACTOR = 2


def rms_norm(hidden, gain):
    hid32 = hidden.astype(jnp.float32)
    return hid32 * lax.rsqrt(jnp.mean(hid32 * hid32, axis=-1, keepdims=True) + NORM_EPS) * gain


def attention(hidden, pad_mask, rel_bias, gain, query_w, key_w, value_w, out_w):
    num_seqs, seq_len, model_dim = hidden.shape
    num_heads = rel_bias.shape[0]
    head_dim = query_w.shape[1] // num_heads
    normed = rms_norm(hidden, gain).astype(jnp.bfloat16)

    def project(weight):
        out_rows = jnp.einsum('std,de->ste', normed, weight, preferred_element_type=jnp.float32)
        return out_rows.astype(jnp.bfloat16).reshape(num_seqs, seq_len, num_heads, head_dim)

    query_rows = project(query_w)
    key_rows = project(key_w)
    value_rows = project(value_w)
    scores = jnp.einsum('sqhd,skhd->shqk', query_rows, key_rows, preferred_element_type=jnp.float32)
    scores = scores + rel_bias[None] + jnp.where(pad_mask > 0, 0.0, NEG_BIG)[:, None, None, :]
    attn_probs = jax.nn.softmax(scores, axis=-1).astype(jnp.bfloat16)
    context = jnp.einsum('shqk,skhd->sqhd', attn_probs, value_rows, preferred_element_type=jnp.float32)
    context = context.astype(jnp.bfloat16).reshape(num_seqs, seq_len, num_heads * head_dim)
    attn_out = jnp.einsum('ste,ed->std', context, out_w, preferred_element_type=jnp.float32)
    return (hidden.astype(jnp.float32) + attn_out).astype(jnp.bfloat16)


def token_slots(expert_ids, num_experts):
    tok_count = expert_ids.shape[0]
    sort_order = jnp.argsort(expert_ids, stable=True)
    counts = jnp.zeros((num_experts,), jnp.int32).at[expert_ids].add(1)
    starts = jnp.cumsum(counts) - counts
    rank_sorted = jnp.arange(tok_count, dtype=jnp.int32) - starts[expert_ids[sort_order]]
    return jnp.zeros((tok_count,), jnp.int32).at[sort_order].set(rank_sorted)


def dispatch(flat_hidden, expert_ids, gain, route_w, capacity):
    tok_count, model_dim = flat_hidden.shape
    num_experts = route_w.shape[1]
    normed32 = rms_norm(flat_hidden, gain)
    logits = jnp.dot(normed32, route_w, precision=lax.Precision.HIGHEST, preferred_element_type=jnp.float32)
    gate_val = jnp.take_along_axis(jax.nn.softmax(logits, axis=-1), expert_ids[:, None], axis=1)[:, 0]
    token_slot = token_slots(expert_ids, num_experts)
    flat_slot = jnp.where(token_slot < capacity, expert_ids * capacity + token_slot, num_experts * capacity)
    slot_token = jnp.full((num_experts * capacity,), tok_count, jnp.int32).at[flat_slot].set(jnp.arange(tok_count, dtype=jnp.int32), mode='drop')
    packed = jnp.take(normed32.astype(jnp.bfloat16), slot_token, axis=0, mode='fill', fill_value=0)
    return packed.reshape(num_experts, capacity, model_dim), gate_val, flat_slot


def expert_ffn(rows_in, up_w, down_w):
    inner_act = jnp.einsum('ecd,edf->ecf', rows_in, up_w, preferred_element_type=jnp.float32)
    inner_act = jnp.maximum(inner_act, 0.0).astype(jnp.bfloat16)
    return jnp.einsum('ecf,efd->ecd', inner_act, down_w, preferred_element_type=jnp.float32).astype(jnp.bfloat16)


def combine(flat_hidden, expert_rows, gate_val, flat_slot):
    returned = jnp.take(expert_rows, flat_slot, axis=0, mode='fill', fill_value=0)
    return (flat_hidden.astype(jnp.float32) + gate_val[:, None] * returned.astype(jnp.float32)).astype(jnp.bfloat16)


def solution(mesh):
    token_spec = P(('dp', 'ep'))

    def per_device(x_in, pad_mask, rel_bias, expert_idx, norm_scale, w_query, w_key, w_value, w_attn_out, w_router, w_in, w_out):
        num_seqs, seq_len, model_dim = x_in.shape
        tok_count = num_seqs * seq_len
        num_experts = w_router.shape[2]
        capacity = (CAP_FACTOR * tok_count + num_experts - 1) // num_experts
        hidden = x_in
        for layer_id in range(w_router.shape[0]):
            hidden = attention(hidden, pad_mask, rel_bias, norm_scale[layer_id, 0], w_query[layer_id], w_key[layer_id], w_value[layer_id], w_attn_out[layer_id])
            flat_hidden = hidden.reshape(tok_count, model_dim)
            packed, gate_val, flat_slot = dispatch(flat_hidden, expert_idx[layer_id].reshape(tok_count), norm_scale[layer_id, 1], w_router[layer_id], capacity)
            received = lax.all_to_all(packed, 'ep', 0, 1, tiled=True)
            expert_rows = expert_ffn(received, w_in[layer_id], w_out[layer_id])
            returned = lax.all_to_all(expert_rows, 'ep', 1, 0, tiled=True)
            hidden = combine(flat_hidden, returned.reshape(num_experts * capacity, model_dim), gate_val, flat_slot).reshape(num_seqs, seq_len, model_dim)
        return hidden

    return jax.shard_map(per_device, mesh=mesh, in_specs=(token_spec, token_spec, P(), P(None, ('dp', 'ep')), P(), P(), P(), P(), P(), P(), P(None, 'ep'), P(None, 'ep')), out_specs=token_spec, check_vma=False)
```

profile of v0, /device:TPU:103, one launch (start us, length us, event | category | flops | bytes accessed | tf_op | source)
XLA Modules:
  0.0 1461.3 jit_solution(11649381006563475105)
XLA Ops:
  36.5 35.5 %select_subtract_fusion.1 = s32[1536]{0:T(1024)S(1)} fusion(pred[1536]{0:T(1024)(128)(4,1)S(1)} %get-tuple-element.127, pred[1536]{0:T(1024)(128)(4,1)S(1)} %get-tuple-element.126, pred[1536]{0:T(1024)(128)(4,1)S(1)} %get-tuple-element.125, pred[1536]{0:T(1024)(128)(4,1)S(1)} %get-tuple-element.124, pred[1536]{0:T(1024)(128)(4,1)S(1)} %get-tuple-element.123, ...), kind=kLoop, calls=%fused_computation.280 | loop fusion | flops 89088 | bytes 100068 | tf_op jit(solution)/shard_map/sub | solution.py:43
  92.3 19.1 %convert_bitcast_fusion.3 = bf16[3,64,16,8,128]{4,3,2,1,0:T(8,128)(2,1)} fusion(bf16[2,2048,2048]{2,1,0:T(8,128)(2,1)} %param.23, bf16[3,512,2048]{2,1,0:T(8,128)(2,1)} %param.18, f32[2048]{0:T(1024)S(1)} %bitcast.338, f32[3,512]{1,0:T(4,128)S(1)} %add_rsqrt_fusion.3), kind=kOutput, calls=%fused_computation.112 | convolution fusion | flops 12900630528 | bytes 20985856 | tf_op jit(solution)/shard_map/std,de->ste/dot_general | solution.py:23
  111.5 18.3 %convert_bitcast_fusion.2 = bf16[3,64,16,8,128]{4,3,2,1,0:T(8,128)(2,1)} fusion(bf16[2,2048,2048]{2,1,0:T(8,128)(2,1)} %param.24, bf16[3,512,2048]{2,1,0:T(8,128)(2,1)S(1)} %bitcast.323, f32[2048]{0:T(1024)S(1)} %bitcast.339, f32[3,512]{1,0:T(4,128)S(1)} %add_rsqrt_fusion.3), kind=kOutput, calls=%fused_computation.111 | convolution fusion | flops 12900630528 | bytes 20985856 | tf_op jit(solution)/shard_map/std,de->ste/dot_general | solution.py:23
  129.8 18.2 %fusion.75 = bf16[3,512,2048]{2,1,0:T(8,128)(2,1)} fusion(bf16[2,2048,2048]{2,1,0:T(8,128)(2,1)} %param.25, bf16[3,512,2048]{2,1,0:T(8,128)(2,1)S(1)} %bitcast.323, f32[2048]{0:T(1024)S(1)} %bitcast.340, f32[3,512]{1,0:T(4,128)S(1)} %add_rsqrt_fusion.3), kind=kOutput, calls=%fused_computation.113 | convolution fusion | flops 12900630528 | bytes 20985856 | tf_op jit(solution)/shard_map/std,de->ste/dot_general | solution.py:23
  156.5 17.6 %copy.62 = f32[16,512,512]{1,2,0:T(8,128)} copy(f32[16,512,512]{2,1,0:T(8,128)} %param.20) | data formatting | bytes 33554432 | tf_op args[2]
  174.1 21.7 %fusion.68 = f32[3,16,512,512]{2,3,1,0:T(8,128)} fusion(bf16[3,64,16,8,128]{4,3,2,1,0:T(8,128)(2,1)} %convert_bitcast_fusion.2, bf16[3,64,16,8,128]{4,3,2,1,0:T(8,128)(2,1)} %convert_bitcast_fusion.3), kind=kOutput, calls=%fused_computation.104 | convolution fusion | flops 3221225472 | bytes 62914560 | tf_op jit(solution)/shard_map/sqhd,skhd->shqk/dot_general | solution.py:29
  195.8 60.7 %fusion.148 = (f32[3,16,512]{2,1,0:T(8,128)S(1)}, f32[3,16,512,512]{2,3,1,0:T(8,128)}) fusion(f32[3,16,512,512]{2,3,1,0:T(8,128)} %fusion.68, f32[3,512]{1,0:T(4,128)S(1)} %compare_select_fusion.22, f32[16,512,512]{1,2,0:T(8,128)} %copy.62), kind=kOutput, calls=%fused_computation.331 | output fusion | flops 75497984 | bytes 117544960 | tf_op jit(solution)/shard_map/sub | solution.py:31
  256.6 22.3 %fusion.92 = bf16[3,16,128,512]{3,2,1,0:T(8,128)(2,1)} fusion(bf16[3,512,16,128]{1,3,2,0:T(8,128)(2,1)} %bitcast.325, f32[3,16,512,512]{2,3,1,0:T(8,128)} %get-tuple-element.279, f32[3,16,512]{2,1,0:T(8,128)S(1)} %get-tuple-element.278), kind=kOutput, calls=%fused_computation.116 | convolution fusion | flops 3249537024 | bytes 63012864 | tf_op jit(solution)/shard_map/shqk,skhd->sqhd/dot_general | solution.py:32
  278.8 21.1 %fusion.19 = (f32[3,512]{1,0:T(4,128)S(1)}, bf16[3,512,2048]{2,1,0:T(8,128)(2,1)}) fusion(bf16[3,512,2048]{1,2,0:T(8,128)(2,1)} %bitcast.346, bf16[2,2048,2048]{2,1,0:T(8,128)(2,1)} %param.26, bf16[3,512,2048]{2,1,0:T(8,128)(2,1)} %param.18), kind=kOutput, calls=%fused_computation.50 | convolution fusion | flops 12903774208 | bytes 27269120 | tf_op jit(solution)/shard_map/ste,ed->std/dot_general | solution.py:34
  307.0 27.4 %gather_fusion.3 = bf16[3072,2048]{1,0:T(8,128)(2,1)} fusion(bf16[1536,2048]{1,0:T(8,128)(2,1)} %fusion.22, s32[3072]{0:T(1024)S(1)} %copy-done.12), kind=kCustom, calls=%fused_computation.1.clone | custom fusion | bytes 25178112 | tf_op jit(solution)/shard_map/jit(_take)/gather | solution.py:56
  341.7 160.0 %all_to_all.66 = bf16[64,48,2048]{2,1,0:T(8,128)(2,1)S(1)} all-to-all(bf16[64,48,2048]{2,1,0:T(8,128)(2,1)S(1)} %bitcast.315), channel_id=1, replica_groups=mesh['dp'=1,'ep'=32] {'ep'}, dimensions={0} | all-to-all | bytes 25165824 | tf_op jit(solution)/shard_map/all_to_all | solution.py:84
  503.7 17.5 %maximum_convert_fusion.1 = bf16[2,1536,1024]{2,1,0:T(8,128)(2,1)} fusion(bf16[2,1536,2048]{2,1,0:T(8,128)(2,1)S(1)} %bitcast.320, bf16[2,2,2048,1024]{3,2,1,0:T(8,128)(2,1)} %param.28), kind=kOutput, calls=%fused_computation.59 | convolution fusion | flops 12891193344 | bytes 27262976 | tf_op jit(solution)/shard_map/ecd,edf->ecf/dot_general | solution.py:61
  521.2 20.3 %convolution_convert_fusion.1 = bf16[2,1536,2048]{2,1,0:T(8,128)(2,1)} fusion(bf16[2,1536,1024]{2,1,0:T(8,128)(2,1)} %maximum_convert_fusion.1, bf16[2,2,1024,2048]{3,2,1,0:T(8,128)(2,1)} %param.29), kind=kOutput, calls=%fused_computation.63 | convolution fusion | flops 12891193344 | bytes 27262976 | tf_op jit(solution)/shard_map/ecf,efd->ecd/dot_general | solution.py:63
  541.5 23.7 %copy.68 = bf16[2,1536,2048]{2,0,1:T(2,128)(2,1)} copy(bf16[2,1536,2048]{2,1,0:T(8,128)(2,1)} %convolution_convert_fusion.1) | data formatting | bytes 25165824 | tf_op jit(solution)/shard_map/convert_element_type | solution.py:63
  606.5 35.5 %select_subtract_fusion = s32[1536]{0:T(1024)S(1)} fusion(pred[1536]{0:T(1024)(128)(4,1)S(1)} %get-tuple-element.70, pred[1536]{0:T(1024)(128)(4,1)S(1)} %get-tuple-element.69, pred[1536]{0:T(1024)(128)(4,1)S(1)} %get-tuple-element.68, pred[1536]{0:T(1024)(128)(4,1)S(1)} %get-tuple-element.67, pred[1536]{0:T(1024)(128)(4,1)S(1)} %get-tuple-element.66, ...), kind=kLoop, calls=%fused_computation.279 | loop fusion | flops 89088 | bytes 100068 | tf_op jit(solution)/shard_map/sub | solution.py:43
  687.0 53.7 %all-to-all-done.1 = bf16[2,1536,2048]{2,0,1:T(2,128)(2,1)} async-done(((bf16[2,1536,2048]{2,0,1:T(2,128)(2,1)}), bf16[2,1536,2048]{2,0,1:T(2,128)(2,1)}, u32[]{:S(2)}, u32[]{:S(2)}) %all-to-all-start.1) | async-done | bytes 12582944 | tf_op jit(solution)/shard_map/all_to_all | solution.py:86
  754.0 18.9 %gather_fusion.4 = bf16[1536,2048]{1,0:T(8,128)(2,1)} fusion(bf16[3072,2048]{1,0:T(8,128)(2,1)} %bitcast.311, s32[2048]{0:T(1024)S(1)} %pad_clamp_fusion.2), kind=kCustom, calls=%fused_computation.2.clone | custom fusion | bytes 12589056 | tf_op jit(solution)/shard_map/jit(_take)/gather | solution.py:67
  793.2 19.0 %convert_bitcast_fusion = bf16[3,64,16,8,128]{4,3,2,1,0:T(8,128)(2,1)} fusion(bf16[3,512,2048]{2,1,0:T(8,128)(2,1)} %bitcast.326, bf16[2,2048,2048]{2,1,0:T(8,128)(2,1)} %param.24), kind=kOutput, calls=%fused_computation.109 | convolution fusion | flops 12888047616 | bytes 20971520 | tf_op jit(solution)/shard_map/std,de->ste/dot_general | solution.py:23
  812.2 15.3 %convert_bitcast_fusion.1 = bf16[3,64,16,8,128]{4,3,2,1,0:T(8,128)(2,1)} fusion(bf16[3,512,2048]{2,1,0:T(8,128)(2,1)S(1)} %bitcast.327, bf16[2,2048,2048]{2,1,0:T(8,128)(2,1)S(1)} %bitcast.344), kind=kOutput, calls=%fused_computation.110 | convolution fusion | flops 12888047616 | bytes 20971520 | tf_op jit(solution)/shard_map/std,de->ste/dot_general | solution.py:23
  827.5 17.3 %fusion.82 = bf16[3,512,2048]{2,1,0:T(8,128)(2,1)} fusion(bf16[3,512,2048]{2,1,0:T(8,128)(2,1)S(1)} %bitcast.328, bf16[2,2048,2048]{2,1,0:T(8,128)(2,1)} %param.25), kind=kOutput, calls=%fused_computation.114 | convolution fusion | flops 12888047616 | bytes 20971520 | tf_op jit(solution)/shard_map/std,de->ste/dot_general | solution.py:23
  853.5 21.7 %fusion.63 = f32[3,16,512,512]{2,3,1,0:T(8,128)} fusion(bf16[3,64,16,8,128]{4,3,2,1,0:T(8,128)(2,1)} %convert_bitcast_fusion, bf16[3,64,16,8,128]{4,3,2,1,0:T(8,128)(2,1)} %convert_bitcast_fusion.1), kind=kOutput, calls=%fused_computation.99 | convolution fusion | flops 3221225472 | bytes 62914560 | tf_op jit(solution)/shard_map/sqhd,skhd->shqk/dot_general | solution.py:29
  875.2 61.1 %fusion.150 = (f32[3,16,512]{2,1,0:T(8,128)S(1)}, f32[3,16,512,512]{2,3,1,0:T(8,128)}) fusion(f32[3,16,512,512]{2,3,1,0:T(8,128)} %fusion.63, f32[3,512]{1,0:T(4,128)S(1)} %copy-done.2, f32[16,512,512]{1,2,0:T(8,128)} %copy.62), kind=kOutput, calls=%fused_computation.333 | output fusion | flops 75497984 | bytes 117544960 | tf_op jit(solution)/shard_map/sub | solution.py:31
  936.4 22.1 %fusion.91 = bf16[3,16,128,512]{3,2,1,0:T(8,128)(2,1)} fusion(bf16[3,512,16,128]{1,3,2,0:T(8,128)(2,1)} %bitcast.324, f32[3,16,512,512]{2,3,1,0:T(8,128)} %get-tuple-element.285, f32[3,16,512]{2,1,0:T(8,128)S(1)} %get-tuple-element.284), kind=kOutput, calls=%fused_computation.115 | convolution fusion | flops 3249537024 | bytes 63012864 | tf_op jit(solution)/shard_map/shqk,skhd->sqhd/dot_general | solution.py:32
  958.4 22.1 %fusion.14 = (f32[3,512]{1,0:T(4,128)S(1)}, bf16[3,512,2048]{2,1,0:T(8,128)(2,1)}) fusion(f32[3,512,2048]{2,1,0:T(8,128)} %bitcast.319, bf16[3,512,2048]{1,2,0:T(8,128)(2,1)} %bitcast.345, bf16[2,2048,2048]{2,1,0:T(8,128)(2,1)} %param.26), kind=kOutput, calls=%fused_computation.41 | convolution fusion | flops 12900628480 | bytes 33560576 | tf_op jit(solution)/shard_map/ste,ed->std/dot_general | solution.py:34
  987.5 27.4 %gather_fusion.6 = bf16[3072,2048]{1,0:T(8,128)(2,1)} fusion(bf16[1536,2048]{1,0:T(8,128)(2,1)} %fusion.17, s32[3072]{0:T(1024)S(1)} %copy-done.11), kind=kCustom, calls=%fused_computation.4.clone | custom fusion | bytes 25178112 | tf_op jit(solution)/shard_map/jit(_take)/gather | solution.py:56
  1021.8 152.2 %all_to_all.67 = bf16[64,48,2048]{2,1,0:T(8,128)(2,1)S(1)} all-to-all(bf16[64,48,2048]{2,1,0:T(8,128)(2,1)S(1)} %bitcast.316), channel_id=1, replica_groups=mesh['dp'=1,'ep'=32] {'ep'}, dimensions={0} | all-to-all | bytes 25165824 | tf_op jit(solution)/shard_map/all_to_all | solution.py:84
  1176.0 17.5 %maximum_convert_fusion = bf16[2,1536,1024]{2,1,0:T(8,128)(2,1)} fusion(bf16[2,1536,2048]{2,1,0:T(8,128)(2,1)S(1)} %bitcast.321, bf16[2,2,2048,1024]{3,2,1,0:T(8,128)(2,1)} %param.28), kind=kOutput, calls=%fused_computation.55 | convolution fusion | flops 12891193344 | bytes 27262976 | tf_op jit(solution)/shard_map/ecd,edf->ecf/dot_general | solution.py:61
  1193.5 20.3 %convolution_convert_fusion = bf16[2,1536,2048]{2,1,0:T(8,128)(2,1)} fusion(bf16[2,1536,1024]{2,1,0:T(8,128)(2,1)} %maximum_convert_fusion, bf16[2,2,1024,2048]{3,2,1,0:T(8,128)(2,1)} %param.29), kind=kOutput, calls=%fused_computation.62 | convolution fusion | flops 12891193344 | bytes 27262976 | tf_op jit(solution)/shard_map/ecf,efd->ecd/dot_general | solution.py:63
  1213.8 23.7 %copy.77 = bf16[2,1536,2048]{2,0,1:T(2,128)(2,1)} copy(bf16[2,1536,2048]{2,1,0:T(8,128)(2,1)} %convolution_convert_fusion) | data formatting | bytes 25165824 | tf_op jit(solution)/shard_map/convert_element_type | solution.py:63
  1280.1 139.2 %all-to-all-done.3 = bf16[2,1536,2048]{2,0,1:T(2,128)(2,1)} async-done(((bf16[2,1536,2048]{2,0,1:T(2,128)(2,1)}), bf16[2,1536,2048]{2,0,1:T(2,128)(2,1)}, u32[]{:S(2)}, u32[]{:S(2)}) %all-to-all-start.3) | async-done | bytes 12582944 | tf_op jit(solution)/shard_map/all_to_all | solution.py:86
  1419.3 13.5 copy.78
  1432.8 18.9 %gather_fusion.7 = bf16[1536,2048]{1,0:T(8,128)(2,1)} fusion(bf16[3072,2048]{1,0:T(8,128)(2,1)} %bitcast.312, s32[2048]{0:T(1024)S(1)} %pad_clamp_fusion), kind=kCustom, calls=%fused_computation.5.clone | custom fusion | bytes 12589056 | tf_op jit(solution)/shard_map/jit(_take)/gather | solution.py:67
  (160 shorter events, 277.3 us)
Async XLA Ops:
  0.0 91.7 %copy-start.16 = (f32[2,2,2048]{2,1,0:T(2,128)S(1)}, f32[2,2,2048]{2,1,0:T(2,128)}, u32[]{:S(2)}) copy-start(f32[2,2,2048]{2,1,0:T(2,128)} %param.22) | copy-start | bytes 98308
  3.2 11.1 copy-start.27
  78.8 32.7 %copy-start.17 = (s32[1536]{0:T(1024)}, s32[1536]{0:T(1024)S(1)}, u32[]{:S(2)}) copy-start(s32[1536]{0:T(1024)S(1)} %get-tuple-element.135) | copy-start | bytes 18436
  87.4 108.4 %copy-start.1 = (f32[3,512]{1,0:T(4,128)}, f32[3,512]{1,0:T(4,128)S(1)}, u32[]{:S(2)}) copy-start(f32[3,512]{1,0:T(4,128)S(1)} %compare_select_fusion.22) | copy-start | bytes 18436
  87.4 24.0 %slice-start = ((s8[6291456]{0:T(1024)(128)(4,1)}), s8[4194304]{0:T(1024)(128)(4,1)S(1)}, s32[]{:S(2)}) async-start(s8[6291456]{0:T(1024)(128)(4,1)} %bitcast.322), calls=%async_computation.4 | async-start | bytes 8388608
  92.3 19.2 %slice-start.1 = ((s8[6291456]{0:T(1024)(128)(4,1)}), s8[2097152]{0:T(1024)(128)(4,1)S(1)}, s32[]{:S(2)}) async-start(s8[6291456]{0:T(1024)(128)(4,1)} %bitcast.322), calls=%async_computation.5 | async-start | bytes 4194304
  278.8 21.2 %copy-start.6 = (f32[1,1,2048]{2,1,0:T(1,128)S(1)}, f32[1,1,2048]{2,1,0:T(1,128)}, u32[]{:S(2)}) copy-start(f32[1,1,2048]{2,1,0:T(1,128)} %get-tuple-element.139) | copy-start | bytes 24580
  300.0 7.0 copy-start.12
  307.0 27.4 %copy-start.24 = (pred[3072]{0:T(1024)(128)(4,1)S(1)}, pred[3072]{0:T(1024)(128)(4,1)}, u32[]{:S(2)}) copy-start(pred[3072]{0:T(1024)(128)(4,1)} %compare_and_fusion.1) | copy-start | bytes 9220
  565.2 7.9 copy-start.15
  565.2 90.1 %copy-start.21 = (s32[1536,1,1]{0,2,1:T(1,128)S(1)}, s32[1536,1,1]{0,2,1:T(1,128)}, u32[]{:S(2)}) copy-start(s32[1536,1,1]{0,2,1:T(1,128)} %get-tuple-element.148) | copy-start | bytes 18436
  565.2 90.1 %copy-start.22 = (s32[1536,1,1]{0,2,1:T(1,128)S(1)}, s32[1536,1,1]{0,2,1:T(1,128)}, u32[]{:S(2)}) copy-start(s32[1536,1,1]{0,2,1:T(1,128)} %get-tuple-element.291) | copy-start | bytes 18436
  565.2 175.5 %all-to-all-start.1 = ((bf16[2,1536,2048]{2,0,1:T(2,128)(2,1)}), bf16[2,1536,2048]{2,0,1:T(2,128)(2,1)}, u32[]{:S(2)}, u32[]{:S(2)}) async-start(bf16[2,1536,2048]{2,0,1:T(2,128)(2,1)} %copy.68), calls=%async_computation.1 | async-start | bytes 25165824 | tf_op jit(solution)/shard_map/all_to_all | solution.py:86
  578.2 81.9 %copy-start.3 = (f32[2,2048,64]{1,2,0:T(8,128)S(1)}, f32[2,2048,64]{1,2,0:T(8,128)}, u32[]{:S(2)}) copy-start(f32[2,2048,64]{1,2,0:T(8,128)} %param.27) | copy-start | bytes 3145732
  648.9 23.6 %copy-start.19 = (s32[1536]{0:T(1024)}, s32[1536]{0:T(1024)S(1)}, u32[]{:S(2)}) copy-start(s32[1536]{0:T(1024)S(1)} %get-tuple-element.129) | copy-start | bytes 18436
  660.1 25.7 %copy-start.18 = (s32[1536]{0:T(1024)S(1)}, s32[1536]{0:T(1024)}, u32[]{:S(2)}) copy-start(s32[1536]{0:T(1024)} %copy-done.17) | copy-start | bytes 18436
  660.1 25.7 %copy-start.10 = (s32[1,3,512]{2,0,1:T(1,128)S(1)}, s32[1,3,512]{2,0,1:T(1,128)}, u32[]{:S(2)}) copy-start(s32[1,3,512]{2,0,1:T(1,128)} %copy-done.9) | copy-start | bytes 18436
  754.0 18.9 %copy-start.25 = (pred[1536]{0:T(1024)(128)(4,1)S(1)}, pred[1536]{0:T(1024)(128)(4,1)}, u32[]{:S(2)}) copy-start(pred[1536]{0:T(1024)(128)(4,1)} %get-tuple-element.134) | copy-start | bytes 4612
  772.9 11.7 copy-start.14
  784.6 27.6 %slice-start.2 = ((s8[16777216]{0:T(1024)(128)(4,1)}), s8[4194304]{0:T(1024)(128)(4,1)S(1)}, s32[]{:S(2)}) async-start(s8[16777216]{0:T(1024)(128)(4,1)} %bitcast.343), calls=%async_computation.6 | async-start | bytes 8388608
  793.2 19.0 %copy-start = (bf16[1536,2048]{1,0:T(8,128)(2,1)S(1)}, bf16[1536,2048]{1,0:T(8,128)(2,1)}, u32[]{:S(2)}) copy-start(bf16[1536,2048]{1,0:T(8,128)(2,1)} %multiply_convert_fusion) | copy-start | bytes 18874372
  793.2 19.0 %slice-start.3 = ((s8[16777216]{0:T(1024)(128)(4,1)}), s8[4194304]{0:T(1024)(128)(4,1)S(1)}, s32[]{:S(2)}) async-start(s8[16777216]{0:T(1024)(128)(4,1)} %bitcast.343), calls=%async_computation.7 | async-start | bytes 8388608
  793.2 19.0 %slice-start.4 = ((s8[16777216]{0:T(1024)(128)(4,1)}), s8[4194304]{0:T(1024)(128)(4,1)S(1)}, s32[]{:S(2)}) async-start(s8[16777216]{0:T(1024)(128)(4,1)} %bitcast.343), calls=%async_computation.8 | async-start | bytes 8388608
  793.2 19.0 %slice-start.5 = ((s8[16777216]{0:T(1024)(128)(4,1)}), s8[4194304]{0:T(1024)(128)(4,1)S(1)}, s32[]{:S(2)}) async-start(s8[16777216]{0:T(1024)(128)(4,1)} %bitcast.343), calls=%async_computation.9 | async-start | bytes 8388608
  853.5 21.7 %copy-start.2 = (f32[3,512]{1,0:T(4,128)S(1)}, f32[3,512]{1,0:T(4,128)}, u32[]{:S(2)}) copy-start(f32[3,512]{1,0:T(4,128)} %copy-done.1) | copy-start | bytes 18436
  958.4 22.1 %copy-start.5 = (f32[1,1,2048]{2,1,0:T(1,128)S(1)}, f32[1,1,2048]{2,1,0:T(1,128)}, u32[]{:S(2)}) copy-start(f32[1,1,2048]{2,1,0:T(1,128)} %get-tuple-element.138) | copy-start | bytes 24580
  987.5 27.4 %copy-start.23 = (pred[3072]{0:T(1024)(128)(4,1)S(1)}, pred[3072]{0:T(1024)(128)(4,1)}, u32[]{:S(2)}) copy-start(pred[3072]{0:T(1024)(128)(4,1)} %compare_and_fusion) | copy-start | bytes 9220
  1237.5 13.0 copy-start.20
  1237.5 13.1 copy-start.13
  1237.5 181.8 %all-to-all-start.3 = ((bf16[2,1536,2048]{2,0,1:T(2,128)(2,1)}), bf16[2,1536,2048]{2,0,1:T(2,128)(2,1)}, u32[]{:S(2)}, u32[]{:S(2)}) async-start(bf16[2,1536,2048]{2,0,1:T(2,128)(2,1)} %copy.77), calls=%async_computation.3 | async-start | bytes 25165824 | tf_op jit(solution)/shard_map/all_to_all | solution.py:86
  1254.8 25.2 %copy-start.8 = (s32[1,3,512]{2,0,1:T(1,128)S(1)}, s32[1,3,512]{2,0,1:T(1,128)}, u32[]{:S(2)}) copy-start(s32[1,3,512]{2,0,1:T(1,128)} %copy-done.7) | copy-start | bytes 18436
  1432.8 18.9 %copy-start.26 = (pred[1536]{0:T(1024)(128)(4,1)S(1)}, pred[1536]{0:T(1024)(128)(4,1)}, u32[]{:S(2)}) copy-start(pred[1536]{0:T(1024)(128)(4,1)} %get-tuple-element.128) | copy-start | bytes 4612
  (4 other events, 13.6 us)
where the time goes:
time: 1470 us; the launch traced here: 1460 us
  matrix products  338 us (23%)
  other arithmetic  313 us (21%)
  blocking collectives  312 us (21%)
  local copies, waits for them, and re-layouts  282 us (19%)
  waiting for transfers between devices  193 us (13%)
  starting transfers between devices  20.9 us (1%)
    all_to_all x2, blocking collectives, per_device(): received = lax.all_to_all(packed, 'ep', 0, 1, tiled=True)  312 us
    all_to_all x2, waiting for transfers between devices, per_device(): returned = lax.all_to_all(expert_rows, 'ep', 1, 0, tiled=True)  193 us
    sub x2, other arithmetic, attention(): attn_probs = jax.nn.softmax(scores, axis=-1).astype(jnp.bfloat16)  122 us
    dot_general x6, matrix products, project(): jnp.einsum('std,de->ste', normed, weight, preferred_element_type=jnp.floa...  107 us
    sub x2, other arithmetic, token_slots(): jnp.arange(tok_count, dtype=jnp.int32) - starts[expert_ids[sort_order]]  71 us
    gather x2, local copies, waits for them, and re-layouts, dispatch(): jnp.take(normed32.astype(jnp.bfloat16), slot_token, axis=0, mode='fill',...  54.9 us
    convert_element_type x2, local copies, waits for them, and re-layouts, expert_ffn(): jnp.einsum('ecf,efd->ecd', inner_act, down_w, preferred_element_type=jnp....  47.4 us
    dot_general x2, matrix products, attention(): jnp.einsum('shqk,skhd->sqhd', attn_probs, value_rows, preferred_element_t...  44.3 us
  transfers between devices with their start and end apart: 2, of which 2 were waited for; matrix products, arithmetic and copies ran while one was open for 10% of the time, Pallas kernels for 0%

commit v1 on v0

v1 whole, which is shorter than its diff:
```python
import functools

import jax
import jax.numpy as jnp
from jax import lax
from jax.experimental import pallas as pl
from jax.experimental.pallas import tpu as pltpu
from jax.sharding import PartitionSpec as P

NORM_EPS = 1e-6
NEG_BIG = -1e9
CAP_FACTOR = 2
HEADS_PER_STEP = 2


def rms_norm(hidden, gain):
    hid32 = hidden.astype(jnp.float32)
    return hid32 * lax.rsqrt(jnp.mean(hid32 * hid32, axis=-1, keepdims=True) + NORM_EPS) * gain


def attn_kernel(head_dim, q_ref, k_ref, v_ref, bias_ref, mask_ref, o_ref):
    mask = mask_ref[0]
    for head in range(bias_ref.shape[0]):
        cols = slice(head * head_dim, (head + 1) * head_dim)
        scores = lax.dot_general(q_ref[:, cols], k_ref[:, cols], (((1,), (1,)), ((), ())), preferred_element_type=jnp.float32)
        scores = scores + bias_ref[head] + mask
        top = jnp.max(scores, axis=-1, keepdims=True)
        weights = jnp.exp(scores - top)
        total = jnp.sum(weights, axis=-1, keepdims=True)
        probs = (weights * (1.0 / total)).astype(jnp.bfloat16)
        out = jnp.dot(probs, v_ref[:, cols], preferred_element_type=jnp.float32)
        o_ref[:, cols] = out.astype(jnp.bfloat16)


def attention_core(query, key, value, rel_bias, mask_add, num_seqs):
    num_heads, seq_len, _ = rel_bias.shape
    head_dim = query.shape[1] // num_heads
    step = HEADS_PER_STEP
    rows = pl.BlockSpec((seq_len, step * head_dim), lambda h, s: (s, h))
    return pl.pallas_call(
        functools.partial(attn_kernel, head_dim),
        grid=(num_heads // step, num_seqs),
        in_specs=[rows, rows, rows, pl.BlockSpec((step, seq_len, seq_len), lambda h, s: (h, 0, 0)), pl.BlockSpec((1, 1, seq_len), lambda h, s: (s, 0, 0))],
        out_specs=rows,
        out_shape=jax.ShapeDtypeStruct(query.shape, jnp.bfloat16),
        compiler_params=pltpu.CompilerParams(vmem_limit_bytes=48 * 1024 * 1024),
        cost_estimate=pl.CostEstimate(flops=4 * num_seqs * seq_len * seq_len * query.shape[1], bytes_accessed=8 * query.size + 4 * rel_bias.size, transcendentals=num_seqs * num_heads * seq_len * seq_len),
        name="attn_core",
    )(query, key, value, rel_bias, mask_add)


def attention(flat, mask_add, rel_bias, gain, query_w, key_w, value_w, out_w, num_seqs):
    normed = rms_norm(flat, gain).astype(jnp.bfloat16)

    def project(weight):
        return jnp.dot(normed, weight, preferred_element_type=jnp.float32).astype(jnp.bfloat16)

    context = attention_core(project(query_w), project(key_w), project(value_w), rel_bias, mask_add, num_seqs)
    attn_out = jnp.dot(context, out_w, preferred_element_type=jnp.float32)
    return (flat.astype(jnp.float32) + attn_out).astype(jnp.bfloat16)


def route_tables(expert_ids, num_experts, capacity):
    tok_count = expert_ids.shape[1]
    member = expert_ids[:, :, None] == jnp.arange(num_experts, dtype=jnp.int32)
    tok = jnp.arange(tok_count, dtype=jnp.int32)
    earlier = (tok[:, None] > tok[None, :]).astype(jnp.bfloat16)
    ranks = jnp.einsum('ts,lse->lte', earlier, member.astype(jnp.bfloat16), preferred_element_type=jnp.float32)
    slot = jnp.sum(jnp.where(member, ranks, 0.0), axis=-1).astype(jnp.int32)
    in_slot = (slot[:, :, None] == jnp.arange(capacity, dtype=jnp.int32)).astype(jnp.bfloat16)
    high = (tok // 32).astype(jnp.bfloat16)[None, :, None] * in_slot
    low = (tok % 32).astype(jnp.bfloat16)[None, :, None] * in_slot
    parts = jnp.einsum('lte,ltc->lec', member.astype(jnp.bfloat16), jnp.concatenate([high, low], axis=-1), preferred_element_type=jnp.float32)
    parts = parts.astype(jnp.int32)
    slot_token = parts[:, :, :capacity] * 32 + parts[:, :, capacity:]
    return member, slot, slot_token


def gate_values(normed32, route_w, member):
    logits = jnp.dot(normed32, route_w, precision=lax.Precision.HIGHEST, preferred_element_type=jnp.float32)
    return jnp.sum(jnp.where(member, jax.nn.softmax(logits, axis=-1), 0.0), axis=-1)


def solution(mesh):
    token_spec = P(('dp', 'ep'))
    groups = mesh.shape['ep']

    def per_device(x_in, pad_mask, rel_bias, expert_idx, norm_scale, w_query, w_key, w_value, w_attn_out, w_router, w_in, w_out):
        num_seqs, seq_len, model_dim = x_in.shape
        tok_count = num_seqs * seq_len
        num_layers, _, num_experts = w_router.shape
        capacity = (CAP_FACTOR * tok_count + num_experts - 1) // num_experts
        local = num_experts // groups
        flat_ids = expert_idx.reshape(num_layers, tok_count)
        member, slot, slot_token = route_tables(flat_ids, num_experts, capacity)
        kept = slot < capacity
        back = (flat_ids // local) * capacity + jnp.minimum(slot, capacity - 1)
        which = flat_ids % local
        mask_add = jnp.where(pad_mask > 0, 0.0, NEG_BIG).astype(jnp.float32)[:, None, :]
        flat = x_in.reshape(tok_count, model_dim)
        for lay in range(num_layers):
            flat = attention(flat, mask_add, rel_bias, norm_scale[lay, 0], w_query[lay], w_key[lay], w_value[lay], w_attn_out[lay], num_seqs)
            normed32 = rms_norm(flat, norm_scale[lay, 1])
            rows = normed32.astype(jnp.bfloat16)
            sources = slot_token[lay].reshape(groups, local, capacity)
            for loc in range(local):
                packed = jnp.take(rows, sources[:, loc].reshape(-1), axis=0, mode='clip')
                received = lax.all_to_all(packed, 'ep', 0, 0, tiled=True)
                inner = jnp.dot(received, w_in[lay, loc], preferred_element_type=jnp.float32)
                inner = jnp.maximum(inner, 0.0).astype(jnp.bfloat16)
                outer = jnp.dot(inner, w_out[lay, loc], preferred_element_type=jnp.float32).astype(jnp.bfloat16)
                returned = lax.all_to_all(outer, 'ep', 0, 0, tiled=True)
                mine = jnp.take(returned, back[lay], axis=0, mode='clip')
                update = jnp.where((which[lay] == loc)[:, None], mine, update) if loc else mine
            gate = gate_values(normed32, w_router[lay], member[lay])
            scale = jnp.where(kept[lay], gate, 0.0)[:, None]
            flat = (flat.astype(jnp.float32) + scale * update.astype(jnp.float32)).astype(jnp.bfloat16)
        return flat.reshape(num_seqs, seq_len, model_dim)

    return jax.shard_map(per_device, mesh=mesh, in_specs=(token_spec, token_spec, P(), P(None, ('dp', 'ep')), P(), P(), P(), P(), P(), P(), P(None, 'ep'), P(None, 'ep')), out_specs=token_spec, check_vma=False)
```

time: 1470 us -> 1050 us (0.71)
  blocking collectives: 312 us -> 0 us
  waiting for transfers between devices: 193 us -> 498 us
  other arithmetic: 313 us -> 38.6 us
  local copies, waits for them, and re-layouts: 282 us -> 139 us
  matrix products: 338 us -> 254 us
  Pallas kernels: 0 us -> 77 us
  starting transfers between devices: 20.9 us -> 37.5 us
    all_to_all x2 -> x0, blocking collectives: 312 us -> none  [per_device(): received = lax.all_to_all(packed, 'ep', 0, 1, tiled=True)]
    all_to_all x2 -> x8, waiting for transfers between devices: 193 us -> 498 us  [the longest x4 266 us: per_device(): received = lax.all_to_all(packed, 'ep', 0, 0, tiled=True)]
    sub x6 -> x0, other arithmetic: 193 us -> none  [the longest x2 122 us: attention(): attn_probs = jax.nn.softmax(scores, axis=-1).astype(jnp.bfloat16)]
    dot_general x18 -> x16, matrix products: 338 us -> 254 us  [the longest x6 107 us: project(): jnp.dot(normed, weight, preferred_element_type=jnp.float32)]
    pallas_call x0 -> x2, Pallas kernels: none -> 77 us  [attention_core(): pl.pallas_call(functools.partial(attn_kernel, head_dim), grid=(num_heads...]
    convert_element_type x2 -> x0, local copies, waits for them, and re-layouts: 47.4 us -> none  [expert_ffn(): jnp.einsum('ecf,efd->ecd', inner_act, down_w, preferred_element_type=jnp....]
    all_to_all x4 -> x0, local copies, waits for them, and re-layouts: 30.6 us -> none  [the longest x2 26.8 us: per_device(): returned = lax.all_to_all(expert_rows, 'ep', 1, 0, tiled=True)]
    scatter x4 -> x0, local copies, waits for them, and re-layouts: 25.5 us -> none  [the longest x2 13.1 us: dispatch(): jnp.full((num_experts * capacity,), tok_count, jnp.int32).at[flat_slot]]
  transfers between devices with their start and end apart: 2 -> 8, of which waited for: 2 -> 8; matrix products, arithmetic and copies ran while one was open for 10% -> 17% of each run, Pallas kernels for 0% -> 0%
where the time goes in v1:
time: 1050 us
  waiting for transfers between devices  498 us (47%)
  matrix products  254 us (24%)
  local copies, waits for them, and re-layouts  139 us (13%)
  Pallas kernels  77 us (7%)
  other arithmetic  38.6 us (4%)
  starting transfers between devices  37.5 us (4%)
    all_to_all x4, waiting for transfers between devices, per_device(): received = lax.all_to_all(packed, 'ep', 0, 0, tiled=True)  266 us
    all_to_all x4, waiting for transfers between devices, per_device(): returned = lax.all_to_all(outer, 'ep', 0, 0, tiled=True)  233 us
    dot_general x6, matrix products, project(): jnp.dot(normed, weight, preferred_element_type=jnp.float32)  107 us
    dot_general x4, matrix products, per_device(): jnp.dot(inner, w_out[lay, loc], preferred_element_type=jnp.float32)  77.4 us
    pallas_call x2, Pallas kernels, attention_core(): pl.pallas_call(functools.partial(attn_kernel, head_dim), grid=(num_heads...  77 us
    gather x4, local copies, waits for them, and re-layouts, per_device(): packed = jnp.take(rows, sources[:, loc].reshape(-1), axis=0, mode='clip')  65.4 us
    gather x4, local copies, waits for them, and re-layouts, per_device(): mine = jnp.take(returned, back[lay], axis=0, mode='clip')  65.2 us
    dot_general x2, matrix products, attention(): attn_out = jnp.dot(context, out_w, preferred_element_type=jnp.float32)  37.5 us
  transfers between devices with their start and end apart: 8, of which 8 were waited for; matrix products, arithmetic and copies ran while one was open for 17% of the time, Pallas kernels for 0%

profile of v1, /device:TPU:103, one launch (start us, length us, event | category | flops | bytes accessed | tf_op | source)
XLA Modules:
  0.0 1045.6 jit_solution(413786961045764126)
XLA Ops:
  12.3 17.7 %fusion.48.v_ref = bf16[1536,2048]{1,0:T(8,128)(2,1)} fusion(bf16[1536,2048]{1,0:T(8,128)(2,1)S(1)} %bitcast.153, bf16[2,2048,2048]{2,1,0:T(8,128)(2,1)} %param.19), kind=kOutput, calls=%fused_computation.66 | convolution fusion | flops 12888047616 | bytes 20971520 | tf_op jit(solution)/shard_map/dot_general | solution.py:56
  30.0 17.7 %fusion.45.k_ref = bf16[1536,2048]{1,0:T(8,128)(2,1)} fusion(bf16[1536,2048]{1,0:T(8,128)(2,1)S(1)} %bitcast.154, bf16[2,2048,2048]{2,1,0:T(8,128)(2,1)} %param.18), kind=kOutput, calls=%fused_computation.65 | convolution fusion | flops 12888047616 | bytes 20971520 | tf_op jit(solution)/shard_map/dot_general | solution.py:56
  47.7 18.0 %fusion.42.q_ref = bf16[1536,2048]{1,0:T(8,128)(2,1)} fusion(bf16[1536,2048]{1,0:T(8,128)(2,1)S(1)} %bitcast.155, bf16[2,2048,2048]{2,1,0:T(8,128)(2,1)} %param.17), kind=kOutput, calls=%fused_computation.64 | convolution fusion | flops 12888047616 | bytes 20971520 | tf_op jit(solution)/shard_map/dot_general | solution.py:56
  65.7 38.5 %attn_core.2 = bf16[1536,2048]{1,0:T(8,128)(2,1)} custom-call(bf16[1536,2048]{1,0:T(8,128)(2,1)} %fusion.42.q_ref, bf16[1536,2048]{1,0:T(8,128)(2,1)} %fusion.45.k_ref, bf16[1536,2048]{1,0:T(8,128)(2,1)} %fusion.48.v_ref, f32[16,512,512]{2,1,0:T(8,128)} %bias_ref.3, f32[3,1,512]{2,1,0:T(1,128)S(1)} %broadcast_in_dim.80.mask_ref), custom_call_target="tpu_custom_call" | custom-call | flops 6442450944 | bytes 41943040 | tf_op jit(solution)/shard_map/attn_core/pallas_call | solution.py:40
  104.3 18.6 %fusion = (f32[1536]{0:T(1024)S(1)}, bf16[1536,2048]{1,0:T(8,128)(2,1)S(1)}) fusion(bf16[1536,2048]{1,0:T(8,128)(2,1)} %attn_core.2, bf16[2,2048,2048]{2,1,0:T(8,128)(2,1)} %param.20, bf16[3,512,2048]{2,1,0:T(8,128)(2,1)S(1)} %bitcast.144), kind=kOutput, calls=%fused_computation.17 | convolution fusion | flops 12903774208 | bytes 27269120 | tf_op jit(solution)/shard_map/dot_general | solution.py:59
  129.7 16.5 %gather_fusion.2 = bf16[1536,2048]{1,0:T(8,128)(2,1)} fusion(bf16[1536,2048]{1,0:T(8,128)(2,1)} %fusion.2, s32[2048]{0:T(1024)S(1)} %pad_clamp_fusion.3), kind=kCustom, calls=%fused_computation.2 | custom fusion | bytes 12589056 | tf_op jit(solution)/shard_map/jit(_take)/gather | solution.py:107
  154.3 16.3 %gather_fusion = bf16[1536,2048]{1,0:T(8,128)(2,1)} fusion(bf16[1536,2048]{1,0:T(8,128)(2,1)} %fusion.2, s32[2048]{0:T(1024)S(1)} %pad_clamp_fusion.5), kind=kCustom, calls=%fused_computation | custom fusion | bytes 12589056 | tf_op jit(solution)/shard_map/jit(_take)/gather | solution.py:107
  170.6 68.0 %all-to-all-done.2 = bf16[32,48,2048]{2,1,0:T(8,128)(2,1)} async-done(((bf16[32,48,2048]{2,1,0:T(8,128)(2,1)}), bf16[32,48,2048]{2,1,0:T(8,128)(2,1)}, u32[]{:S(2)}, u32[]{:S(2)}) %all-to-all-start.2) | async-done | bytes 6291488 | tf_op jit(solution)/shard_map/all_to_all | solution.py:108
  242.7 19.4 %convolution_convert_fusion.2 = bf16[1536,2048]{1,0:T(8,128)(2,1)} fusion(bf16[1536,2048]{1,0:T(8,128)(2,1)} %bitcast.21, bf16[2,2,1024,2048]{3,2,1,0:T(8,128)(2,1)} %param.23, bf16[2,2,2048,1024]{3,2,1,0:T(8,128)(2,1)} %param.22), kind=kOutput, calls=%fused_computation.62 | convolution fusion | flops 12891193344 | bytes 20971520 | tf_op jit(solution)/shard_map/dot_general | solution.py:111
  262.1 65.0 %all-to-all-done = bf16[32,48,2048]{2,1,0:T(8,128)(2,1)} async-done(((bf16[32,48,2048]{2,1,0:T(8,128)(2,1)}), bf16[32,48,2048]{2,1,0:T(8,128)(2,1)}, u32[]{:S(2)}, u32[]{:S(2)}) %all-to-all-start) | async-done | bytes 6291488 | tf_op jit(solution)/shard_map/all_to_all | solution.py:108
  331.1 19.3 %convolution_convert_fusion.3 = bf16[1536,2048]{1,0:T(8,128)(2,1)} fusion(bf16[1536,2048]{1,0:T(8,128)(2,1)} %bitcast.15, bf16[2,2,1024,2048]{3,2,1,0:T(8,128)(2,1)} %param.23, bf16[2,2,2048,1024]{3,2,1,0:T(8,128)(2,1)} %param.22), kind=kOutput, calls=%fused_computation.63 | convolution fusion | flops 12891193344 | bytes 20971520 | tf_op jit(solution)/shard_map/dot_general | solution.py:111
  350.5 65.0 %all-to-all-done.3 = bf16[32,48,2048]{2,1,0:T(8,128)(2,1)} async-done(((bf16[32,48,2048]{2,1,0:T(8,128)(2,1)}), bf16[32,48,2048]{2,1,0:T(8,128)(2,1)}, u32[]{:S(2)}, u32[]{:S(2)}) %all-to-all-start.3) | async-done | bytes 6291488 | tf_op jit(solution)/shard_map/all_to_all | solution.py:112
  422.5 15.1 %fusion.138 = (f32[1536]{0:T(1024)S(1)}, f32[1536,64]{0,1:T(8,128)S(1)}) fusion(f32[2,2048,64]{1,2,0:T(8,128)S(1)} %copy-done.16, bf16[1536,2048]{1,0:T(8,128)(2,1)} %copy-done, f32[2048]{0:T(1024)S(1)} %bitcast.165, f32[1536]{0:T(1024)S(1)} %add_rsqrt_fusion.2), kind=kOutput, calls=%fused_computation.177 | convolution fusion | flops 2425453056 | bytes 7231488 | tf_op jit(solution)/shard_map/dot_general | solution.py:80
  438.4 16.3 %gather_fusion.3 = bf16[1536,2048]{1,0:T(8,128)(2,1)} fusion(bf16[1536,2048]{1,0:T(8,128)(2,1)} %bitcast.25, s32[2048]{0:T(1024)S(1)} %pad_clamp_fusion.4), kind=kCustom, calls=%fused_computation.3 | custom fusion | bytes 12589056 | tf_op jit(solution)/shard_map/jit(_take)/gather | solution.py:113
  454.7 50.3 %all-to-all-done.1 = bf16[32,48,2048]{2,1,0:T(8,128)(2,1)} async-done(((bf16[32,48,2048]{2,1,0:T(8,128)(2,1)}), bf16[32,48,2048]{2,1,0:T(8,128)(2,1)}, u32[]{:S(2)}, u32[]{:S(2)}) %all-to-all-start.1) | async-done | bytes 6291488 | tf_op jit(solution)/shard_map/all_to_all | solution.py:112
  505.0 16.3 %gather_fusion.1 = bf16[1536,2048]{1,0:T(8,128)(2,1)} fusion(bf16[1536,2048]{1,0:T(8,128)(2,1)} %bitcast.19, s32[2048]{0:T(1024)S(1)} %pad_clamp_fusion.4), kind=kCustom, calls=%fused_computation.1 | custom fusion | bytes 12589056 | tf_op jit(solution)/shard_map/jit(_take)/gather | solution.py:113
  530.2 18.0 %fusion.54.k_ref = bf16[1536,2048]{1,0:T(8,128)(2,1)} fusion(bf16[2,2048,2048]{2,1,0:T(8,128)(2,1)} %param.18, bf16[1536,2048]{1,0:T(8,128)(2,1)S(1)} %get-tuple-element.16, f32[2048]{0:T(1024)S(1)} %bitcast.167, f32[1536]{0:T(1024)S(1)} %add_rsqrt_fusion.1), kind=kOutput, calls=%fused_computation.68 | convolution fusion | flops 12900630528 | bytes 20985856 | tf_op jit(solution)/shard_map/dot_general | solution.py:56
  548.2 17.9 %fusion.57.v_ref = bf16[1536,2048]{1,0:T(8,128)(2,1)} fusion(bf16[2,2048,2048]{2,1,0:T(8,128)(2,1)} %param.19, bf16[1536,2048]{1,0:T(8,128)(2,1)S(1)} %get-tuple-element.16, f32[2048]{0:T(1024)S(1)} %bitcast.168, f32[1536]{0:T(1024)S(1)} %add_rsqrt_fusion.1), kind=kOutput, calls=%fused_computation.69 | convolution fusion | flops 12900630528 | bytes 20985856 | tf_op jit(solution)/shard_map/dot_general | solution.py:56
  566.2 18.1 %fusion.51.q_ref = bf16[1536,2048]{1,0:T(8,128)(2,1)} fusion(bf16[2,2048,2048]{2,1,0:T(8,128)(2,1)} %param.17, bf16[1536,2048]{1,0:T(8,128)(2,1)S(1)} %get-tuple-element.16, f32[2048]{0:T(1024)S(1)} %bitcast.169, f32[1536]{0:T(1024)S(1)} %add_rsqrt_fusion.1), kind=kOutput, calls=%fused_computation.67 | convolution fusion | flops 12900630528 | bytes 20985856 | tf_op jit(solution)/shard_map/dot_general | solution.py:56
  584.3 38.5 %attn_core.3 = bf16[1536,2048]{1,0:T(8,128)(2,1)} custom-call(bf16[1536,2048]{1,0:T(8,128)(2,1)} %fusion.51.q_ref, bf16[1536,2048]{1,0:T(8,128)(2,1)} %fusion.54.k_ref, bf16[1536,2048]{1,0:T(8,128)(2,1)} %fusion.57.v_ref, f32[16,512,512]{2,1,0:T(8,128)} %bias_ref.3, f32[3,1,512]{2,1,0:T(1,128)S(1)} %broadcast_in_dim.80.mask_ref), custom_call_target="tpu_custom_call" | custom-call | flops 6442450944 | bytes 41943040 | tf_op jit(solution)/shard_map/attn_core/pallas_call | solution.py:40
  622.8 19.0 %fusion.10 = (f32[1536]{0:T(1024)S(1)}, bf16[1536,2048]{1,0:T(8,128)(2,1)S(1)}) fusion(bf16[1536,2048]{1,0:T(8,128)(2,1)} %attn_core.3, bf16[2,2048,2048]{2,1,0:T(8,128)(2,1)} %param.20, bf16[1536,2048]{1,0:T(8,128)(2,1)S(1)} %get-tuple-element.16), kind=kOutput, calls=%fused_computation.26 | convolution fusion | flops 12903774208 | bytes 27269120 | tf_op jit(solution)/shard_map/dot_general | solution.py:59
  648.6 16.3 %gather_fusion.6 = bf16[1536,2048]{1,0:T(8,128)(2,1)} fusion(bf16[1536,2048]{1,0:T(8,128)(2,1)} %fusion.12, s32[2048]{0:T(1024)S(1)} %pad_clamp_fusion), kind=kCustom, calls=%fused_computation.6 | custom fusion | bytes 12589056 | tf_op jit(solution)/shard_map/jit(_take)/gather | solution.py:107
  668.9 16.3 %gather_fusion.4 = bf16[1536,2048]{1,0:T(8,128)(2,1)} fusion(bf16[1536,2048]{1,0:T(8,128)(2,1)} %fusion.12, s32[2048]{0:T(1024)S(1)} %pad_clamp_fusion.2), kind=kCustom, calls=%fused_computation.4 | custom fusion | bytes 12589056 | tf_op jit(solution)/shard_map/jit(_take)/gather | solution.py:107
  685.2 67.4 %all-to-all-done.6 = bf16[32,48,2048]{2,1,0:T(8,128)(2,1)} async-done(((bf16[32,48,2048]{2,1,0:T(8,128)(2,1)}), bf16[32,48,2048]{2,1,0:T(8,128)(2,1)}, u32[]{:S(2)}, u32[]{:S(2)}) %all-to-all-start.6) | async-done | bytes 6291488 | tf_op jit(solution)/shard_map/all_to_all | solution.py:108
  756.6 19.3 %convolution_convert_fusion = bf16[1536,2048]{1,0:T(8,128)(2,1)} fusion(bf16[1536,2048]{1,0:T(8,128)(2,1)} %bitcast.42, bf16[2,2,1024,2048]{3,2,1,0:T(8,128)(2,1)} %param.23, bf16[2,2,2048,1024]{3,2,1,0:T(8,128)(2,1)} %param.22), kind=kOutput, calls=%fused_computation.60 | convolution fusion | flops 12891193344 | bytes 20971520 | tf_op jit(solution)/shard_map/dot_general | solution.py:111
  775.9 65.2 %all-to-all-done.4 = bf16[32,48,2048]{2,1,0:T(8,128)(2,1)} async-done(((bf16[32,48,2048]{2,1,0:T(8,128)(2,1)}), bf16[32,48,2048]{2,1,0:T(8,128)(2,1)}, u32[]{:S(2)}, u32[]{:S(2)}) %all-to-all-start.4) | async-done | bytes 6291488 | tf_op jit(solution)/shard_map/all_to_all | solution.py:108
  844.9 19.3 %convolution_convert_fusion.1 = bf16[1536,2048]{1,0:T(8,128)(2,1)} fusion(bf16[1536,2048]{1,0:T(8,128)(2,1)} %bitcast.36, bf16[2,2,1024,2048]{3,2,1,0:T(8,128)(2,1)} %param.23, bf16[2,2,2048,1024]{3,2,1,0:T(8,128)(2,1)} %param.22), kind=kOutput, calls=%fused_computation.61 | convolution fusion | flops 12891193344 | bytes 20971520 | tf_op jit(solution)/shard_map/dot_general | solution.py:111
  864.2 64.6 %all-to-all-done.7 = bf16[32,48,2048]{2,1,0:T(8,128)(2,1)} async-done(((bf16[32,48,2048]{2,1,0:T(8,128)(2,1)}), bf16[32,48,2048]{2,1,0:T(8,128)(2,1)}, u32[]{:S(2)}, u32[]{:S(2)}) %all-to-all-start.7) | async-done | bytes 6291488 | tf_op jit(solution)/shard_map/all_to_all | solution.py:112
  933.6 15.1 %fusion.139 = (f32[1536]{0:T(1024)S(1)}, f32[1536,64]{0,1:T(8,128)S(1)}) fusion(f32[2,2048,64]{1,2,0:T(8,128)S(1)} %copy-done.17, bf16[1536,2048]{1,0:T(8,128)(2,1)} %copy-done.1, f32[2048]{0:T(1024)S(1)} %bitcast.163, f32[1536]{0:T(1024)S(1)} %add_rsqrt_fusion), kind=kOutput, calls=%fused_computation.178 | convolution fusion | flops 2425453056 | bytes 7231488 | tf_op jit(solution)/shard_map/dot_general | solution.py:80
  949.0 16.3 %gather_fusion.7 = bf16[1536,2048]{1,0:T(8,128)(2,1)} fusion(bf16[1536,2048]{1,0:T(8,128)(2,1)} %bitcast.46, s32[2048]{0:T(1024)S(1)} %pad_clamp_fusion.1), kind=kCustom, calls=%fused_computation.7 | custom fusion | bytes 12589056 | tf_op jit(solution)/shard_map/jit(_take)/gather | solution.py:113
  965.3 52.9 %all-to-all-done.5 = bf16[32,48,2048]{2,1,0:T(8,128)(2,1)} async-done(((bf16[32,48,2048]{2,1,0:T(8,128)(2,1)}), bf16[32,48,2048]{2,1,0:T(8,128)(2,1)}, u32[]{:S(2)}, u32[]{:S(2)}) %all-to-all-start.5) | async-done | bytes 6291488 | tf_op jit(solution)/shard_map/all_to_all | solution.py:112
  1018.2 16.3 %gather_fusion.5 = bf16[1536,2048]{1,0:T(8,128)(2,1)} fusion(bf16[1536,2048]{1,0:T(8,128)(2,1)} %bitcast.40, s32[2048]{0:T(1024)S(1)} %pad_clamp_fusion.1), kind=kCustom, calls=%fused_computation.5 | custom fusion | bytes 12589056 | tf_op jit(solution)/shard_map/jit(_take)/gather | solution.py:113
  (93 shorter events, 86.4 us)
Async XLA Ops:
  0.0 4.8 copy-start.8
  0.0 6.1 copy-start.12
  6.1 1.9 copy-start.4
  30.0 74.3 %slice-start = ((s8[6291456]{0:T(1024)(128)(4,1)}), s8[4194304]{0:T(1024)(128)(4,1)S(1)}, s32[]{:S(2)}) async-start(s8[6291456]{0:T(1024)(128)(4,1)} %bitcast.143), calls=%async_computation.8 | async-start | bytes 8388608
  47.7 56.6 %slice-start.1 = ((s8[6291456]{0:T(1024)(128)(4,1)}), s8[2097152]{0:T(1024)(128)(4,1)S(1)}, s32[]{:S(2)}) async-start(s8[6291456]{0:T(1024)(128)(4,1)} %bitcast.143), calls=%async_computation.9 | async-start | bytes 4194304
  122.8 2.7 copy-start
  146.2 92.4 %all-to-all-start.2 = ((bf16[32,48,2048]{2,1,0:T(8,128)(2,1)}), bf16[32,48,2048]{2,1,0:T(8,128)(2,1)}, u32[]{:S(2)}, u32[]{:S(2)}) async-start(bf16[32,48,2048]{2,1,0:T(8,128)(2,1)} %bitcast.148), calls=%async_computation.2 | async-start | bytes 12582912 | tf_op jit(solution)/shard_map/all_to_all | solution.py:108
  238.6 88.4 %all-to-all-start = ((bf16[32,48,2048]{2,1,0:T(8,128)(2,1)}), bf16[32,48,2048]{2,1,0:T(8,128)(2,1)}, u32[]{:S(2)}, u32[]{:S(2)}) async-start(bf16[32,48,2048]{2,1,0:T(8,128)(2,1)} %bitcast.145), calls=%async_computation | async-start | bytes 12582912 | tf_op jit(solution)/shard_map/all_to_all | solution.py:108
  327.1 88.4 %all-to-all-start.3 = ((bf16[32,48,2048]{2,1,0:T(8,128)(2,1)}), bf16[32,48,2048]{2,1,0:T(8,128)(2,1)}, u32[]{:S(2)}, u32[]{:S(2)}) async-start(bf16[32,48,2048]{2,1,0:T(8,128)(2,1)} %bitcast.151), calls=%async_computation.3 | async-start | bytes 12582912 | tf_op jit(solution)/shard_map/all_to_all | solution.py:112
  415.5 4.9 copy-start.7
  415.5 5.0 copy-start.5
  415.5 5.0 copy-start.9
  415.5 7.0 copy-start.16
  415.5 89.5 %all-to-all-start.1 = ((bf16[32,48,2048]{2,1,0:T(8,128)(2,1)}), bf16[32,48,2048]{2,1,0:T(8,128)(2,1)}, u32[]{:S(2)}, u32[]{:S(2)}) async-start(bf16[32,48,2048]{2,1,0:T(8,128)(2,1)} %bitcast.149), calls=%async_computation.1 | async-start | bytes 12582912 | tf_op jit(solution)/shard_map/all_to_all | solution.py:112
  437.7 0.7 copy-start.2
  521.3 8.9 copy-start.15
  622.8 21.7 %copy-start.10 = (f32[1,1,2048]{2,1,0:T(1,128)S(1)}, f32[1,1,2048]{2,1,0:T(1,128)}, u32[]{:S(2)}) copy-start(f32[1,1,2048]{2,1,0:T(1,128)} %get-tuple-element.19) | copy-start | bytes 24580
  641.8 2.7 copy-start.1
  664.9 4.0 copy-start.6
  664.9 87.7 %all-to-all-start.6 = ((bf16[32,48,2048]{2,1,0:T(8,128)(2,1)}), bf16[32,48,2048]{2,1,0:T(8,128)(2,1)}, u32[]{:S(2)}, u32[]{:S(2)}) async-start(bf16[32,48,2048]{2,1,0:T(8,128)(2,1)} %bitcast.146), calls=%async_computation.6 | async-start | bytes 12582912 | tf_op jit(solution)/shard_map/all_to_all | solution.py:108
  752.6 88.5 %all-to-all-start.4 = ((bf16[32,48,2048]{2,1,0:T(8,128)(2,1)}), bf16[32,48,2048]{2,1,0:T(8,128)(2,1)}, u32[]{:S(2)}, u32[]{:S(2)}) async-start(bf16[32,48,2048]{2,1,0:T(8,128)(2,1)} %bitcast.147), calls=%async_computation.4 | async-start | bytes 12582912 | tf_op jit(solution)/shard_map/all_to_all | solution.py:108
  841.1 87.7 %all-to-all-start.7 = ((bf16[32,48,2048]{2,1,0:T(8,128)(2,1)}), bf16[32,48,2048]{2,1,0:T(8,128)(2,1)}, u32[]{:S(2)}, u32[]{:S(2)}) async-start(bf16[32,48,2048]{2,1,0:T(8,128)(2,1)} %bitcast.152), calls=%async_computation.7 | async-start | bytes 12582912 | tf_op jit(solution)/shard_map/all_to_all | solution.py:112
  928.8 4.8 copy-start.11
  928.8 4.8 copy-start.17
  928.8 89.4 %all-to-all-start.5 = ((bf16[32,48,2048]{2,1,0:T(8,128)(2,1)}), bf16[32,48,2048]{2,1,0:T(8,128)(2,1)}, u32[]{:S(2)}, u32[]{:S(2)}) async-start(bf16[32,48,2048]{2,1,0:T(8,128)(2,1)} %bitcast.150), calls=%async_computation.5 | async-start | bytes 12582912 | tf_op jit(solution)/shard_map/all_to_all | solution.py:112
  933.6 15.2 %copy-start.3 = (pred[2,1536,64]{1,2,0:T(8,128)(4,1)S(1)}, pred[2,1536,64]{1,2,0:T(8,128)(4,1)}, u32[]{:S(2)}) copy-start(pred[2,1536,64]{1,2,0:T(8,128)(4,1)} %copy-done.2) | copy-start | bytes 589828
  933.6 15.3 %copy-start.14 = (pred[1536]{0:T(1024)(128)(4,1)S(1)}, pred[1536]{0:T(1024)(128)(4,1)}, u32[]{:S(2)}) copy-start(pred[1536]{0:T(1024)(128)(4,1)} %get-tuple-element.13) | copy-start | bytes 4612
  1018.2 16.3 %copy-start.13 = (pred[1536]{0:T(1024)(128)(4,1)S(1)}, pred[1536]{0:T(1024)(128)(4,1)}, u32[]{:S(2)}) copy-start(pred[1536]{0:T(1024)(128)(4,1)} %get-tuple-element.9) | copy-start | bytes 4612

commit v2 on v1

--- a/solution.py
+++ b/solution.py
@@ -10,7 +10,7 @@
 NORM_EPS = 1e-6
 NEG_BIG = -1e9
 CAP_FACTOR = 2
-HEADS_PER_STEP = 2
+HEADS_PER_STEP = 4
 
 
 def rms_norm(hidden, gain):
@@ -20,16 +20,27 @@
 
 def attn_kernel(head_dim, q_ref, k_ref, v_ref, bias_ref, mask_ref, o_ref):
     mask = mask_ref[0]
-    for head in range(bias_ref.shape[0]):
+    heads = bias_ref.shape[0]
+
+    def score(head):
         cols = slice(head * head_dim, (head + 1) * head_dim)
-        scores = lax.dot_general(q_ref[:, cols], k_ref[:, cols], (((1,), (1,)), ((), ())), preferred_element_type=jnp.float32)
-        scores = scores + bias_ref[head] + mask
-        top = jnp.max(scores, axis=-1, keepdims=True)
-        weights = jnp.exp(scores - top)
-        total = jnp.sum(weights, axis=-1, keepdims=True)
-        probs = (weights * (1.0 / total)).astype(jnp.bfloat16)
-        out = jnp.dot(probs, v_ref[:, cols], preferred_element_type=jnp.float32)
-        o_ref[:, cols] = out.astype(jnp.bfloat16)
+        return lax.dot_general(q_ref[:, cols], k_ref[:, cols], (((1,), (1,)), ((), ())), preferred_element_type=jnp.float32)
+
+    ahead = score(0)
+    prev = None
+    for head in range(heads + 1):
+        if head < heads:
+            scores = ahead + bias_ref[head] + mask
+            if head + 1 < heads:
+                ahead = score(head + 1)
+            top = jnp.max(scores, axis=-1, keepdims=True)
+            weights = jnp.exp(scores - top)
+            total = jnp.sum(weights, axis=-1, keepdims=True)
+            probs = (weights * (1.0 / total)).astype(jnp.bfloat16)
+        if prev is not None:
+            cols = slice((head - 1) * head_dim, head * head_dim)
+            o_ref[:, cols] = jnp.dot(prev, v_ref[:, cols], preferred_element_type=jnp.float32).astype(jnp.bfloat16)
+        prev = probs
 
 
 def attention_core(query, key, value, rel_bias, mask_add, num_seqs):
@@ -67,13 +78,7 @@
     earlier = (tok[:, None] > tok[None, :]).astype(jnp.bfloat16)
     ranks = jnp.einsum('ts,lse->lte', earlier, member.astype(jnp.bfloat16), preferred_element_type=jnp.float32)
     slot = jnp.sum(jnp.where(member, ranks, 0.0), axis=-1).astype(jnp.int32)
-    in_slot = (slot[:, :, None] == jnp.arange(capacity, dtype=jnp.int32)).astype(jnp.bfloat16)
-    high = (tok // 32).astype(jnp.bfloat16)[None, :, None] * in_slot
-    low = (tok % 32).astype(jnp.bfloat16)[None, :, None] * in_slot
-    parts = jnp.einsum('lte,ltc->lec', member.astype(jnp.bfloat16), jnp.concatenate([high, low], axis=-1), preferred_element_type=jnp.float32)
-    parts = parts.astype(jnp.int32)
-    slot_token = parts[:, :, :capacity] * 32 + parts[:, :, capacity:]
-    return member, slot, slot_token
+    return member, slot
 
 
 def gate_values(normed32, route_w, member):
@@ -92,29 +97,32 @@
         capacity = (CAP_FACTOR * tok_count + num_experts - 1) // num_experts
         local = num_experts // groups
         flat_ids = expert_idx.reshape(num_layers, tok_count)
-        member, slot, slot_token = route_tables(flat_ids, num_experts, capacity)
-        kept = slot < capacity
-        back = (flat_ids // local) * capacity + jnp.minimum(slot, capacity - 1)
+        member, slot = route_tables(flat_ids, num_experts, capacity)
+        row = jnp.where(slot < capacity, (flat_ids // local) * capacity + slot, -1)
         which = flat_ids % local
+        row_ids = jnp.arange(groups * capacity, dtype=jnp.int32)
         mask_add = jnp.where(pad_mask > 0, 0.0, NEG_BIG).astype(jnp.float32)[:, None, :]
         flat = x_in.reshape(tok_count, model_dim)
         for lay in range(num_layers):
             flat = attention(flat, mask_add, rel_bias, norm_scale[lay, 0], w_query[lay], w_key[lay], w_value[lay], w_attn_out[lay], num_seqs)
             normed32 = rms_norm(flat, norm_scale[lay, 1])
             rows = normed32.astype(jnp.bfloat16)
-            sources = slot_token[lay].reshape(groups, local, capacity)
+            update = None
             for loc in range(local):
-                packed = jnp.take(rows, sources[:, loc].reshape(-1), axis=0, mode='clip')
+                place = jnp.where(which[lay] == loc, row[lay], -1)
+                moves = (row_ids[:, None] == place[None, :]).astype(jnp.bfloat16)
+                packed = jnp.dot(moves, rows, preferred_element_type=jnp.float32).astype(jnp.bfloat16)
                 received = lax.all_to_all(packed, 'ep', 0, 0, tiled=True)
                 inner = jnp.dot(received, w_in[lay, loc], preferred_element_type=jnp.float32)
                 inner = jnp.maximum(inner, 0.0).astype(jnp.bfloat16)
                 outer = jnp.dot(inner, w_out[lay, loc], preferred_element_type=jnp.float32).astype(jnp.bfloat16)
                 returned = lax.all_to_all(outer, 'ep', 0, 0, tiled=True)
-                mine = jnp.take(returned, back[lay], axis=0, mode='clip')
-                update = jnp.where((which[lay] == loc)[:, None], mine, update) if loc else mine
+                mine = lax.dot_general(moves, returned, (((0,), (0,)), ((), ())), preferred_element_type=jnp.float32)
+                update = mine if update is None else update.astype(jnp.float32) + mine
+                if loc < local - 1:
+                    update = update.astype(jnp.bfloat16)
             gate = gate_values(normed32, w_router[lay], member[lay])
-            scale = jnp.where(kept[lay], gate, 0.0)[:, None]
-            flat = (flat.astype(jnp.float32) + scale * update.astype(jnp.float32)).astype(jnp.bfloat16)
+            flat = (flat.astype(jnp.float32) + gate[:, None] * update).astype(jnp.bfloat16)
         return flat.reshape(num_seqs, seq_len, model_dim)
 
     return jax.shard_map(per_device, mesh=mesh, in_specs=(token_spec, token_spec, P(), P(None, ('dp', 'ep')), P(), P(), P(), P(), P(), P(), P(None, 'ep'), P(None, 'ep')), out_specs=token_spec, check_vma=False)

time: 1050 us -> 991 us (0.944)
  local copies, waits for them, and re-layouts: 139 us -> 1.29 us
  matrix products: 254 us -> 371 us
  other arithmetic: 38.6 us -> 8.23 us
  Pallas kernels: 77 us -> 57.9 us
  waiting for transfers between devices: 498 us -> 509 us
    gather x8 -> x0, local copies, waits for them, and re-layouts: 131 us -> none  [the longest x4 65.4 us: per_device(): packed = jnp.take(rows, sources[:, loc].reshape(-1), axis=0, mode='clip')]
    dot_general x1 -> x8, matrix products: 0.32 us -> 119 us  [the longest x4 64.5 us: per_device(): lax.dot_general(moves, returned, (((0,), (0,)), ((), ())), preferred_elem...]
    convert_element_type x6 -> x0, other arithmetic: 19.2 us -> none  [the longest x1 10.9 us: per_device(): (flat.astype(jnp.float32) + scale * update.astype(jnp.float32)).astype(jn...]
    pallas_call x2, Pallas kernels: 77 us -> 57.9 us  [attention_core(): pl.pallas_call(functools.partial(attn_kernel, head_dim), grid=(num_heads...]
where the time goes in v2:
time: 991 us; the launch traced here: 987 us
  waiting for transfers between devices  509 us (51%)
  matrix products  371 us (37%)
  Pallas kernels  57.9 us (6%)
  starting transfers between devices  38.7 us (4%)
    all_to_all x4, waiting for transfers between devices, per_device(): received = lax.all_to_all(packed, 'ep', 0, 0, tiled=True)  270 us
    all_to_all x4, waiting for transfers between devices, per_device(): returned = lax.all_to_all(outer, 'ep', 0, 0, tiled=True)  239 us
    dot_general x6, matrix products, project(): jnp.dot(normed, weight, preferred_element_type=jnp.float32)  107 us
    dot_general x4, matrix products, per_device(): jnp.dot(inner, w_out[lay, loc], preferred_element_type=jnp.float32)  77.4 us
    dot_general x4, matrix products, per_device(): lax.dot_general(moves, returned, (((0,), (0,)), ((), ())), preferred_elem...  64.5 us
    pallas_call x2, Pallas kernels, attention_core(): pl.pallas_call(functools.partial(attn_kernel, head_dim), grid=(num_heads...  57.9 us
    dot_general x4, matrix products, per_device(): jnp.dot(moves, rows, preferred_element_type=jnp.float32)  54.4 us
    dot_general x2, matrix products, attention(): attn_out = jnp.dot(context, out_w, preferred_element_type=jnp.float32)  37.2 us
  transfers between devices with their start and end apart: 8, of which 8 were waited for; matrix products, arithmetic and copies ran while one was open for 17% of the time, Pallas kernels for 0%

profile of v2, /device:TPU:103, one launch (start us, length us, event | category | flops | bytes accessed | tf_op | source)
XLA Modules:
  0.0 987.4 jit_solution(12459421271591440049)
XLA Ops:
  8.8 18.0 %fusion.62.v_ref = bf16[1536,2048]{1,0:T(8,128)(2,1)} fusion(bf16[1536,2048]{1,0:T(8,128)(2,1)S(1)} %bitcast.155, bf16[2,2048,2048]{2,1,0:T(8,128)(2,1)} %param.19), kind=kOutput, calls=%fused_computation.76 | convolution fusion | flops 12888047616 | bytes 20971520 | tf_op jit(solution)/shard_map/dot_general | solution.py:67
  26.9 17.5 %fusion.59.k_ref = bf16[1536,2048]{1,0:T(8,128)(2,1)} fusion(bf16[1536,2048]{1,0:T(8,128)(2,1)S(1)} %bitcast.156, bf16[2,2048,2048]{2,1,0:T(8,128)(2,1)} %param.18), kind=kOutput, calls=%fused_computation.75 | convolution fusion | flops 12888047616 | bytes 20971520 | tf_op jit(solution)/shard_map/dot_general | solution.py:67
  44.4 17.6 %fusion.56.q_ref = bf16[1536,2048]{1,0:T(8,128)(2,1)} fusion(bf16[1536,2048]{1,0:T(8,128)(2,1)S(1)} %bitcast.157, bf16[2,2048,2048]{2,1,0:T(8,128)(2,1)} %param.17), kind=kOutput, calls=%fused_computation.74 | convolution fusion | flops 12888047616 | bytes 20971520 | tf_op jit(solution)/shard_map/dot_general | solution.py:67
  62.1 29.0 %attn_core.2 = bf16[1536,2048]{1,0:T(8,128)(2,1)} custom-call(bf16[1536,2048]{1,0:T(8,128)(2,1)} %fusion.56.q_ref, bf16[1536,2048]{1,0:T(8,128)(2,1)} %fusion.59.k_ref, bf16[1536,2048]{1,0:T(8,128)(2,1)} %fusion.62.v_ref, f32[16,512,512]{2,1,0:T(8,128)} %bias_ref.3, f32[3,1,512]{2,1,0:T(1,128)S(1)} %broadcast_in_dim.30.mask_ref), custom_call_target="tpu_custom_call" | custom-call | flops 6442450944 | bytes 41943040 | tf_op jit(solution)/shard_map/attn_core/pallas_call | solution.py:51
  91.0 18.5 %fusion = (f32[1536]{0:T(1024)S(1)}, bf16[1536,2048]{1,0:T(8,128)(2,1)S(1)}) fusion(bf16[1536,2048]{1,0:T(8,128)(2,1)} %attn_core.2, bf16[2,2048,2048]{2,1,0:T(8,128)(2,1)} %param.20, bf16[3,512,2048]{2,1,0:T(8,128)(2,1)S(1)} %bitcast.146), kind=kOutput, calls=%fused_computation.9 | convolution fusion | flops 12903774208 | bytes 27269120 | tf_op jit(solution)/shard_map/dot_general | solution.py:70
  110.4 12.9 %fusion.50 = bf16[1536,2048]{1,0:T(8,128)(2,1)} fusion(s32[1536]{0:T(1024)S(1)} %get-tuple-element.8, bf16[1536,2048]{1,0:T(8,128)(2,1)S(1)} %get-tuple-element.16, f32[2048]{0:T(1024)S(1)} %bitcast.168, f32[1536]{0:T(1024)S(1)} %add_rsqrt_fusion.2), kind=kOutput, calls=%fused_computation.64 | convolution fusion | flops 9681764352 | bytes 12603392 | tf_op jit(solution)/shard_map/dot_general | solution.py:114
  131.2 14.3 %fusion.52 = bf16[1536,2048]{1,0:T(8,128)(2,1)} fusion(s32[1536]{0:T(1024)S(1)} %get-tuple-element.6, bf16[1536,2048]{1,0:T(8,128)(2,1)} %copy-done.13, f32[2048]{0:T(1024)S(1)} %bitcast.169, f32[1536]{0:T(1024)S(1)} %add_rsqrt_fusion.2), kind=kOutput, calls=%fused_computation.66 | convolution fusion | flops 9681764352 | bytes 12603392 | tf_op jit(solution)/shard_map/dot_general | solution.py:114
  145.6 70.1 %all-to-all-done = bf16[32,48,2048]{2,1,0:T(8,128)(2,1)} async-done(((bf16[32,48,2048]{2,1,0:T(8,128)(2,1)}), bf16[32,48,2048]{2,1,0:T(8,128)(2,1)}, u32[]{:S(2)}, u32[]{:S(2)}) %all-to-all-start) | async-done | bytes 6291488 | tf_op jit(solution)/shard_map/all_to_all | solution.py:115
  220.5 19.4 %convolution_convert_fusion.3 = bf16[1536,2048]{1,0:T(8,128)(2,1)} fusion(bf16[1536,2048]{1,0:T(8,128)(2,1)} %bitcast.14, bf16[2,2,1024,2048]{3,2,1,0:T(8,128)(2,1)} %param.23, bf16[2,2,2048,1024]{3,2,1,0:T(8,128)(2,1)} %param.22), kind=kOutput, calls=%fused_computation.73 | convolution fusion | flops 12891193344 | bytes 20971520 | tf_op jit(solution)/shard_map/dot_general | solution.py:118
  239.9 65.3 %all-to-all-done.2 = bf16[32,48,2048]{2,1,0:T(8,128)(2,1)} async-done(((bf16[32,48,2048]{2,1,0:T(8,128)(2,1)}), bf16[32,48,2048]{2,1,0:T(8,128)(2,1)}, u32[]{:S(2)}, u32[]{:S(2)}) %all-to-all-start.2) | async-done | bytes 6291488 | tf_op jit(solution)/shard_map/all_to_all | solution.py:115
  308.9 19.4 %convolution_convert_fusion.2 = bf16[1536,2048]{1,0:T(8,128)(2,1)} fusion(bf16[1536,2048]{1,0:T(8,128)(2,1)} %bitcast.20, bf16[2,2,1024,2048]{3,2,1,0:T(8,128)(2,1)} %param.23, bf16[2,2,2048,1024]{3,2,1,0:T(8,128)(2,1)} %param.22), kind=kOutput, calls=%fused_computation.72 | convolution fusion | flops 12891193344 | bytes 20971520 | tf_op jit(solution)/shard_map/dot_general | solution.py:118
  328.3 64.5 %all-to-all-done.1 = bf16[32,48,2048]{2,1,0:T(8,128)(2,1)} async-done(((bf16[32,48,2048]{2,1,0:T(8,128)(2,1)}), bf16[32,48,2048]{2,1,0:T(8,128)(2,1)}, u32[]{:S(2)}, u32[]{:S(2)}) %all-to-all-start.1) | async-done | bytes 6291488 | tf_op jit(solution)/shard_map/all_to_all | solution.py:119
  398.0 15.1 %fusion.149 = (f32[1536]{0:T(1024)S(1)}, f32[1536,64]{0,1:T(8,128)S(1)}) fusion(f32[2,2048,64]{1,2,0:T(8,128)S(1)} %copy-done.11, bf16[1536,2048]{1,0:T(8,128)(2,1)} %copy-done.13, f32[2048]{0:T(1024)S(1)} %bitcast.170, f32[1536]{0:T(1024)S(1)} %add_rsqrt_fusion.2), kind=kOutput, calls=%fused_computation.158 | convolution fusion | flops 2425453056 | bytes 7231488 | tf_op jit(solution)/shard_map/dot_general | solution.py:85
  413.9 14.0 %fusion.51 = bf16[1536,2048]{1,0:T(8,128)(2,1)} fusion(bf16[1536,2048]{1,0:T(8,128)(2,1)} %bitcast.18, s32[1536]{0:T(1024)S(1)} %get-tuple-element.8), kind=kOutput, calls=%fused_computation.65 | convolution fusion | flops 9669181440 | bytes 12589056 | tf_op jit(solution)/shard_map/dot_general | solution.py:120
  427.9 54.6 %all-to-all-done.3 = bf16[32,48,2048]{2,1,0:T(8,128)(2,1)} async-done(((bf16[32,48,2048]{2,1,0:T(8,128)(2,1)}), bf16[32,48,2048]{2,1,0:T(8,128)(2,1)}, u32[]{:S(2)}, u32[]{:S(2)}) %all-to-all-start.3) | async-done | bytes 6291488 | tf_op jit(solution)/shard_map/all_to_all | solution.py:119
  482.6 18.7 %fusion.6 = (f32[1536]{0:T(1024)S(1)}, bf16[1536,2048]{1,0:T(8,128)(2,1)}) fusion(bf16[1536,2048]{1,0:T(8,128)(2,1)} %bitcast.24, s32[1536]{0:T(1024)S(1)} %get-tuple-element.6, bf16[1536,2048]{1,0:T(8,128)(2,1)} %fusion.51, f32[1536]{0:T(1024)S(1)} %select_reduce_fusion.1, bf16[1536,2048]{1,0:T(8,128)(2,1)} %copy-done.13), kind=kOutput, calls=%fused_computation.14 | convolution fusion | flops 9694345216 | bytes 25184256 | tf_op jit(solution)/shard_map/dot_general | solution.py:120
  501.3 19.4 %fusion.68.k_ref = bf16[1536,2048]{1,0:T(8,128)(2,1)} fusion(bf16[2,2048,2048]{2,1,0:T(8,128)(2,1)} %param.18, bf16[1536,2048]{1,0:T(8,128)(2,1)} %get-tuple-element.20, f32[2048]{0:T(1024)S(1)} %bitcast.165, f32[1536]{0:T(1024)S(1)} %add_rsqrt_fusion.1), kind=kOutput, calls=%fused_computation.78 | convolution fusion | flops 12900630528 | bytes 20985856 | tf_op jit(solution)/shard_map/dot_general | solution.py:67
  520.7 15.5 %fusion.71.v_ref = bf16[1536,2048]{1,0:T(8,128)(2,1)} fusion(bf16[2,2048,2048]{2,1,0:T(8,128)(2,1)S(1)} %bitcast.172, bf16[1536,2048]{1,0:T(8,128)(2,1)S(1)} %copy-done.15, f32[2048]{0:T(1024)S(1)} %bitcast.166, f32[1536]{0:T(1024)S(1)} %add_rsqrt_fusion.1), kind=kOutput, calls=%fused_computation.79 | convolution fusion | flops 12900630528 | bytes 20987904 | tf_op jit(solution)/shard_map/dot_general | solution.py:67
  536.2 18.5 %fusion.65.q_ref = bf16[1536,2048]{1,0:T(8,128)(2,1)} fusion(bf16[2,2048,2048]{2,1,0:T(8,128)(2,1)} %param.17, bf16[1536,2048]{1,0:T(8,128)(2,1)S(1)} %copy-done.15, f32[2048]{0:T(1024)S(1)} %bitcast.167, f32[1536]{0:T(1024)S(1)} %add_rsqrt_fusion.1), kind=kOutput, calls=%fused_computation.77 | convolution fusion | flops 12900630528 | bytes 20985856 | tf_op jit(solution)/shard_map/dot_general | solution.py:67
  554.7 29.0 %attn_core.3 = bf16[1536,2048]{1,0:T(8,128)(2,1)} custom-call(bf16[1536,2048]{1,0:T(8,128)(2,1)} %fusion.65.q_ref, bf16[1536,2048]{1,0:T(8,128)(2,1)} %fusion.68.k_ref, bf16[1536,2048]{1,0:T(8,128)(2,1)} %fusion.71.v_ref, f32[16,512,512]{2,1,0:T(8,128)} %bias_ref.3, f32[3,1,512]{2,1,0:T(1,128)S(1)} %copy-done.1), custom_call_target="tpu_custom_call" | custom-call | flops 6442450944 | bytes 41943040 | tf_op jit(solution)/shard_map/attn_core/pallas_call | solution.py:51
  583.7 18.7 %fusion.10 = (f32[1536]{0:T(1024)S(1)}, bf16[1536,2048]{1,0:T(8,128)(2,1)S(1)}) fusion(bf16[1536,2048]{1,0:T(8,128)(2,1)} %attn_core.3, bf16[2,2048,2048]{2,1,0:T(8,128)(2,1)} %param.20, bf16[1536,2048]{1,0:T(8,128)(2,1)} %get-tuple-element.20), kind=kOutput, calls=%fused_computation.18 | convolution fusion | flops 12903774208 | bytes 27269120 | tf_op jit(solution)/shard_map/dot_general | solution.py:70
  602.5 12.9 %fusion.53 = bf16[1536,2048]{1,0:T(8,128)(2,1)} fusion(s32[1536]{0:T(1024)S(1)} %copy-done.8, bf16[1536,2048]{1,0:T(8,128)(2,1)S(1)} %get-tuple-element.22, f32[2048]{0:T(1024)S(1)} %bitcast.162, f32[1536]{0:T(1024)S(1)} %add_rsqrt_fusion), kind=kOutput, calls=%fused_computation.67 | convolution fusion | flops 9681764352 | bytes 12603392 | tf_op jit(solution)/shard_map/dot_general | solution.py:114
  619.3 14.3 %fusion.55 = bf16[1536,2048]{1,0:T(8,128)(2,1)} fusion(s32[1536]{0:T(1024)S(1)} %copy-done.7, bf16[1536,2048]{1,0:T(8,128)(2,1)} %copy-done.14, f32[2048]{0:T(1024)S(1)} %bitcast.163, f32[1536]{0:T(1024)S(1)} %add_rsqrt_fusion), kind=kOutput, calls=%fused_computation.69 | convolution fusion | flops 9681764352 | bytes 12603392 | tf_op jit(solution)/shard_map/dot_general | solution.py:114
  633.6 69.4 %all-to-all-done.4 = bf16[32,48,2048]{2,1,0:T(8,128)(2,1)} async-done(((bf16[32,48,2048]{2,1,0:T(8,128)(2,1)}), bf16[32,48,2048]{2,1,0:T(8,128)(2,1)}, u32[]{:S(2)}, u32[]{:S(2)}) %all-to-all-start.4) | async-done | bytes 6291488 | tf_op jit(solution)/shard_map/all_to_all | solution.py:115
  707.1 19.4 %convolution_convert_fusion.1 = bf16[1536,2048]{1,0:T(8,128)(2,1)} fusion(bf16[1536,2048]{1,0:T(8,128)(2,1)} %bitcast.34, bf16[2,2,1024,2048]{3,2,1,0:T(8,128)(2,1)} %param.23, bf16[2,2,2048,1024]{3,2,1,0:T(8,128)(2,1)} %param.22), kind=kOutput, calls=%fused_computation.71 | convolution fusion | flops 12891193344 | bytes 20971520 | tf_op jit(solution)/shard_map/dot_general | solution.py:118
  726.4 65.2 %all-to-all-done.6 = bf16[32,48,2048]{2,1,0:T(8,128)(2,1)} async-done(((bf16[32,48,2048]{2,1,0:T(8,128)(2,1)}), bf16[32,48,2048]{2,1,0:T(8,128)(2,1)}, u32[]{:S(2)}, u32[]{:S(2)}) %all-to-all-start.6) | async-done | bytes 6291488 | tf_op jit(solution)/shard_map/all_to_all | solution.py:115
  795.4 19.3 %convolution_convert_fusion = bf16[1536,2048]{1,0:T(8,128)(2,1)} fusion(bf16[1536,2048]{1,0:T(8,128)(2,1)} %bitcast.40, bf16[2,2,1024,2048]{3,2,1,0:T(8,128)(2,1)} %param.23, bf16[2,2,2048,1024]{3,2,1,0:T(8,128)(2,1)} %param.22), kind=kOutput, calls=%fused_computation.70 | convolution fusion | flops 12891193344 | bytes 20971520 | tf_op jit(solution)/shard_map/dot_general | solution.py:118
  814.7 64.6 %all-to-all-done.5 = bf16[32,48,2048]{2,1,0:T(8,128)(2,1)} async-done(((bf16[32,48,2048]{2,1,0:T(8,128)(2,1)}), bf16[32,48,2048]{2,1,0:T(8,128)(2,1)}, u32[]{:S(2)}, u32[]{:S(2)}) %all-to-all-start.5) | async-done | bytes 6291488 | tf_op jit(solution)/shard_map/all_to_all | solution.py:119
  884.5 15.1 %fusion.150 = (f32[1536]{0:T(1024)S(1)}, f32[1536,64]{0,1:T(8,128)S(1)}) fusion(f32[2,2048,64]{1,2,0:T(8,128)S(1)} %copy-done.12, bf16[1536,2048]{1,0:T(8,128)(2,1)} %copy-done.14, f32[2048]{0:T(1024)S(1)} %bitcast.164, f32[1536]{0:T(1024)S(1)} %add_rsqrt_fusion), kind=kOutput, calls=%fused_computation.159 | convolution fusion | flops 2425453056 | bytes 7231488 | tf_op jit(solution)/shard_map/dot_general | solution.py:85
  899.8 14.0 %fusion.54 = bf16[1536,2048]{1,0:T(8,128)(2,1)} fusion(bf16[1536,2048]{1,0:T(8,128)(2,1)} %bitcast.38, s32[1536]{0:T(1024)S(1)} %copy-done.8), kind=kOutput, calls=%fused_computation.68 | convolution fusion | flops 9669181440 | bytes 12589056 | tf_op jit(solution)/shard_map/dot_general | solution.py:120
  913.8 55.3 %all-to-all-done.7 = bf16[32,48,2048]{2,1,0:T(8,128)(2,1)} async-done(((bf16[32,48,2048]{2,1,0:T(8,128)(2,1)}), bf16[32,48,2048]{2,1,0:T(8,128)(2,1)}, u32[]{:S(2)}, u32[]{:S(2)}) %all-to-all-start.7) | async-done | bytes 6291488 | tf_op jit(solution)/shard_map/all_to_all | solution.py:119
  969.1 17.8 %fusion.15 = bf16[1536,2048]{1,0:T(8,128)(2,1)} fusion(bf16[1536,2048]{1,0:T(8,128)(2,1)} %copy-done.14, bf16[1536,2048]{1,0:T(8,128)(2,1)} %fusion.54, bf16[1536,2048]{1,0:T(8,128)(2,1)} %bitcast.44, f32[1536]{0:T(1024)S(1)} %select_reduce_fusion, s32[1536]{0:T(1024)S(1)} %copy-done.7), kind=kOutput, calls=%fused_computation.22 | convolution fusion | flops 9684910080 | bytes 25178112 | tf_op jit(solution)/shard_map/dot_general | solution.py:120
  (71 shorter events, 49.4 us)
Async XLA Ops:
  0.0 7.3 slice-start
  0.0 5.4 copy-start.4
  0.0 6.7 copy-start.6
  0.9 61.2 %copy-start = (f32[3,1,512]{2,1,0:T(1,128)}, f32[3,1,512]{2,1,0:T(1,128)S(1)}, u32[]{:S(2)}) copy-start(f32[3,1,512]{2,1,0:T(1,128)S(1)} %broadcast_in_dim.30.mask_ref) | copy-start | bytes 18436
  0.9 6.5 slice-start.1
  109.5 13.7 %copy-start.13 = (bf16[1536,2048]{1,0:T(8,128)(2,1)}, bf16[1536,2048]{1,0:T(8,128)(2,1)S(1)}, u32[]{:S(2)}) copy-start(bf16[1536,2048]{1,0:T(8,128)(2,1)S(1)} %get-tuple-element.16) | copy-start | bytes 18874372
  123.2 92.4 %all-to-all-start = ((bf16[32,48,2048]{2,1,0:T(8,128)(2,1)}), bf16[32,48,2048]{2,1,0:T(8,128)(2,1)}, u32[]{:S(2)}, u32[]{:S(2)}) async-start(bf16[32,48,2048]{2,1,0:T(8,128)(2,1)} %bitcast.154), calls=%async_computation | async-start | bytes 12582912 | tf_op jit(solution)/shard_map/all_to_all | solution.py:115
  215.6 89.5 %all-to-all-start.2 = ((bf16[32,48,2048]{2,1,0:T(8,128)(2,1)}), bf16[32,48,2048]{2,1,0:T(8,128)(2,1)}, u32[]{:S(2)}, u32[]{:S(2)}) async-start(bf16[32,48,2048]{2,1,0:T(8,128)(2,1)} %bitcast.151), calls=%async_computation.2 | async-start | bytes 12582912 | tf_op jit(solution)/shard_map/all_to_all | solution.py:115
  305.1 87.7 %all-to-all-start.1 = ((bf16[32,48,2048]{2,1,0:T(8,128)(2,1)}), bf16[32,48,2048]{2,1,0:T(8,128)(2,1)}, u32[]{:S(2)}, u32[]{:S(2)}) async-start(bf16[32,48,2048]{2,1,0:T(8,128)(2,1)} %bitcast.149), calls=%async_computation.1 | async-start | bytes 12582912 | tf_op jit(solution)/shard_map/all_to_all | solution.py:119
  392.8 5.1 copy-start.11
  392.8 89.7 %all-to-all-start.3 = ((bf16[32,48,2048]{2,1,0:T(8,128)(2,1)}), bf16[32,48,2048]{2,1,0:T(8,128)(2,1)}, u32[]{:S(2)}, u32[]{:S(2)}) async-start(bf16[32,48,2048]{2,1,0:T(8,128)(2,1)} %bitcast.147), calls=%async_computation.3 | async-start | bytes 12582912 | tf_op jit(solution)/shard_map/all_to_all | solution.py:119
  397.9 15.2 %copy-start.5 = (s32[2,3,512]{2,0,1:T(2,128)S(1)}, s32[2,3,512]{2,0,1:T(2,128)}, u32[]{:S(2)}) copy-start(s32[2,3,512]{2,0,1:T(2,128)} %param.15) | copy-start | bytes 36868
  413.2 0.7 copy-start.2
  482.5 18.8 %copy-start.10 = (f32[1,1,2048]{2,1,0:T(1,128)S(1)}, f32[1,1,2048]{2,1,0:T(1,128)}, u32[]{:S(2)}) copy-start(f32[1,1,2048]{2,1,0:T(1,128)} %get-tuple-element.12) | copy-start | bytes 24580
  482.5 38.1 %slice-start.2 = ((s8[16777216]{0:T(1024)(128)(4,1)}), s8[4194304]{0:T(1024)(128)(4,1)S(1)}, s32[]{:S(2)}) async-start(s8[16777216]{0:T(1024)(128)(4,1)} %bitcast.171), calls=%async_computation.10 | async-start | bytes 8388608
  482.5 38.1 %slice-start.3 = ((s8[16777216]{0:T(1024)(128)(4,1)}), s8[4194304]{0:T(1024)(128)(4,1)S(1)}, s32[]{:S(2)}) async-start(s8[16777216]{0:T(1024)(128)(4,1)} %bitcast.171), calls=%async_computation.11 | async-start | bytes 8388608
  482.5 38.1 %slice-start.4 = ((s8[16777216]{0:T(1024)(128)(4,1)}), s8[4194304]{0:T(1024)(128)(4,1)S(1)}, s32[]{:S(2)}) async-start(s8[16777216]{0:T(1024)(128)(4,1)} %bitcast.171), calls=%async_computation.12 | async-start | bytes 8388608
  501.3 19.4 %slice-start.5 = ((s8[16777216]{0:T(1024)(128)(4,1)}), s8[4194304]{0:T(1024)(128)(4,1)S(1)}, s32[]{:S(2)}) async-start(s8[16777216]{0:T(1024)(128)(4,1)} %bitcast.171), calls=%async_computation.13 | async-start | bytes 8388608
  501.3 19.4 %copy-start.15 = (bf16[1536,2048]{1,0:T(8,128)(2,1)S(1)}, bf16[1536,2048]{1,0:T(8,128)(2,1)}, u32[]{:S(2)}) copy-start(bf16[1536,2048]{1,0:T(8,128)(2,1)} %get-tuple-element.20) | copy-start | bytes 18874372
  536.2 18.5 %copy-start.1 = (f32[3,1,512]{2,1,0:T(1,128)S(1)}, f32[3,1,512]{2,1,0:T(1,128)}, u32[]{:S(2)}) copy-start(f32[3,1,512]{2,1,0:T(1,128)} %copy-done) | copy-start | bytes 18436
  583.7 18.7 %copy-start.8 = (s32[1536]{0:T(1024)S(1)}, s32[1536]{0:T(1024)}, u32[]{:S(2)}) copy-start(s32[1536]{0:T(1024)} %get-tuple-element.7) | copy-start | bytes 18436
  583.7 18.8 %copy-start.9 = (f32[1,1,2048]{2,1,0:T(1,128)S(1)}, f32[1,1,2048]{2,1,0:T(1,128)}, u32[]{:S(2)}) copy-start(f32[1,1,2048]{2,1,0:T(1,128)} %get-tuple-element.9) | copy-start | bytes 24580
  602.4 12.9 %copy-start.14 = (bf16[1536,2048]{1,0:T(8,128)(2,1)}, bf16[1536,2048]{1,0:T(8,128)(2,1)S(1)}, u32[]{:S(2)}) copy-start(bf16[1536,2048]{1,0:T(8,128)(2,1)S(1)} %get-tuple-element.22) | copy-start | bytes 18874372
  615.3 3.9 copy-start.7
  615.3 87.7 %all-to-all-start.4 = ((bf16[32,48,2048]{2,1,0:T(8,128)(2,1)}), bf16[32,48,2048]{2,1,0:T(8,128)(2,1)}, u32[]{:S(2)}, u32[]{:S(2)}) async-start(bf16[32,48,2048]{2,1,0:T(8,128)(2,1)} %bitcast.153), calls=%async_computation.4 | async-start | bytes 12582912 | tf_op jit(solution)/shard_map/all_to_all | solution.py:115
  703.0 88.5 %all-to-all-start.6 = ((bf16[32,48,2048]{2,1,0:T(8,128)(2,1)}), bf16[32,48,2048]{2,1,0:T(8,128)(2,1)}, u32[]{:S(2)}, u32[]{:S(2)}) async-start(bf16[32,48,2048]{2,1,0:T(8,128)(2,1)} %bitcast.152), calls=%async_computation.6 | async-start | bytes 12582912 | tf_op jit(solution)/shard_map/all_to_all | solution.py:115
  791.6 87.7 %all-to-all-start.5 = ((bf16[32,48,2048]{2,1,0:T(8,128)(2,1)}), bf16[32,48,2048]{2,1,0:T(8,128)(2,1)}, u32[]{:S(2)}, u32[]{:S(2)}) async-start(bf16[32,48,2048]{2,1,0:T(8,128)(2,1)} %bitcast.150), calls=%async_computation.5 | async-start | bytes 12582912 | tf_op jit(solution)/shard_map/all_to_all | solution.py:119
  879.3 5.2 copy-start.12
  879.3 89.8 %all-to-all-start.7 = ((bf16[32,48,2048]{2,1,0:T(8,128)(2,1)}), bf16[32,48,2048]{2,1,0:T(8,128)(2,1)}, u32[]{:S(2)}, u32[]{:S(2)}) async-start(bf16[32,48,2048]{2,1,0:T(8,128)(2,1)} %bitcast.148), calls=%async_computation.7 | async-start | bytes 12582912 | tf_op jit(solution)/shard_map/all_to_all | solution.py:119
  884.5 15.2 %copy-start.3 = (pred[2,1536,64]{1,2,0:T(8,128)(4,1)S(1)}, pred[2,1536,64]{1,2,0:T(8,128)(4,1)}, u32[]{:S(2)}) copy-start(pred[2,1536,64]{1,2,0:T(8,128)(4,1)} %copy-done.2) | copy-start | bytes 589828

commit v3 on v2

--- a/solution.py
+++ b/solution.py
@@ -60,13 +60,42 @@
     )(query, key, value, rel_bias, mask_add)
 
 
-def attention(flat, mask_add, rel_bias, gain, query_w, key_w, value_w, out_w, num_seqs):
-    normed = rms_norm(flat, gain).astype(jnp.bfloat16)
+def project_kernel(hid_ref, gain_ref, query_w, key_w, value_w, query_ref, key_ref, value_ref, normed_ref):
+    tile = 128
 
-    def project(weight):
-        return jnp.dot(normed, weight, preferred_element_type=jnp.float32).astype(jnp.bfloat16)
+    @pl.when(pl.program_id(0) == 0)
+    def _():
+        @pl.loop(0, hid_ref.shape[0] // tile)
+        def _(step):
+            rows = pl.ds(pl.multiple_of(step * tile, tile), tile)
+            normed_ref[rows, :] = rms_norm(hid_ref[rows, :], gain_ref[...]).astype(jnp.bfloat16)
 
-    context = attention_core(project(query_w), project(key_w), project(value_w), rel_bias, mask_add, num_seqs)
+    for weight, out in ((query_w, query_ref), (key_w, key_ref), (value_w, value_ref)):
+        out[...] = jnp.dot(normed_ref[...], weight[0], preferred_element_type=jnp.float32).astype(jnp.bfloat16)
+
+
+def project(layer, flat, gain, query_w, key_w, value_w):
+    tok_count, model_dim = flat.shape
+    inner = query_w.shape[2]
+    cols = 512
+    weight = pl.BlockSpec((1, model_dim, cols), lambda n: (layer, 0, n))
+    out = pl.BlockSpec((tok_count, cols), lambda n: (0, n))
+    return pl.pallas_call(
+        project_kernel,
+        grid=(inner // cols,),
+        in_specs=[pl.BlockSpec((tok_count, model_dim), lambda n: (0, 0), pipeline_mode=pl.Buffered(1)), pl.BlockSpec((1, model_dim), lambda n: (0, 0)), weight, weight, weight],
+        out_specs=(out, out, out),
+        out_shape=(jax.ShapeDtypeStruct((tok_count, inner), jnp.bfloat16),) * 3,
+        scratch_shapes=[pltpu.VMEM((tok_count, model_dim), jnp.bfloat16)],
+        compiler_params=pltpu.CompilerParams(vmem_limit_bytes=56 * 1024 * 1024),
+        cost_estimate=pl.CostEstimate(flops=6 * tok_count * model_dim * inner, bytes_accessed=8 * flat.size + 6 * model_dim * inner, transcendentals=0),
+        name="project",
+    )(flat, gain[None, :], query_w, key_w, value_w)
+
+
+def attention(layer, flat, mask_add, rel_bias, gain, query_w, key_w, value_w, out_w, num_seqs):
+    query, key, value = project(layer, flat, gain, query_w, key_w, value_w)
+    context = attention_core(query, key, value, rel_bias, mask_add, num_seqs)
     attn_out = jnp.dot(context, out_w, preferred_element_type=jnp.float32)
     return (flat.astype(jnp.float32) + attn_out).astype(jnp.bfloat16)
 
@@ -104,7 +133,7 @@
         mask_add = jnp.where(pad_mask > 0, 0.0, NEG_BIG).astype(jnp.float32)[:, None, :]
         flat = x_in.reshape(tok_count, model_dim)
         for lay in range(num_layers):
-            flat = attention(flat, mask_add, rel_bias, norm_scale[lay, 0], w_query[lay], w_key[lay], w_value[lay], w_attn_out[lay], num_seqs)
+            flat = attention(lay, flat, mask_add, rel_bias, norm_scale[lay, 0], w_query, w_key, w_value, w_attn_out[lay], num_seqs)
             normed32 = rms_norm(flat, norm_scale[lay, 1])
             rows = normed32.astype(jnp.bfloat16)
             update = None

time: 991 us -> 983 us (level)
  matrix products: 371 us -> 267 us
  Pallas kernels: 57.9 us -> 157 us
    dot_general x6 -> x0, matrix products: 107 us -> none  [project(): jnp.dot(normed, weight, preferred_element_type=jnp.float32)]
    pallas_call x0 -> x2, Pallas kernels: none -> 98.5 us  [project(): pl.pallas_call(project_kernel, grid=(inner // cols,), in_specs=[pl.BlockS...]
where the time goes in v3:
time: 983 us; the launch traced here: 975 us
  waiting for transfers between devices  508 us (52%)
  matrix products  267 us (27%)
  Pallas kernels  157 us (16%)
  starting transfers between devices  37.7 us (4%)
    all_to_all x4, waiting for transfers between devices, per_device(): received = lax.all_to_all(packed, 'ep', 0, 0, tiled=True)  269 us
    all_to_all x4, waiting for transfers between devices, per_device(): returned = lax.all_to_all(outer, 'ep', 0, 0, tiled=True)  239 us
    pallas_call x2, Pallas kernels, project(): pl.pallas_call(project_kernel, grid=(inner // cols,), in_specs=[pl.BlockS...  98.5 us
    dot_general x4, matrix products, per_device(): jnp.dot(inner, w_out[lay, loc], preferred_element_type=jnp.float32)  77.4 us
    dot_general x4, matrix products, per_device(): lax.dot_general(moves, returned, (((0,), (0,)), ((), ())), preferred_elem...  63.3 us
    pallas_call x2, Pallas kernels, attention_core(): pl.pallas_call(functools.partial(attn_kernel, head_dim), grid=(num_heads...  58.5 us
    dot_general x4, matrix products, per_device(): jnp.dot(moves, rows, preferred_element_type=jnp.float32)  55.7 us
    dot_general x2, matrix products, attention(): attn_out = jnp.dot(context, out_w, preferred_element_type=jnp.float32)  38.3 us
  transfers between devices with their start and end apart: 8, of which 8 were waited for; matrix products, arithmetic and copies ran while one was open for 17% of the time, Pallas kernels for 0%

profile of v3, /device:TPU:103, one launch (start us, length us, event | category | flops | bytes accessed | tf_op | source)
XLA Modules:
  0.0 975.3 jit_solution(6825570770375233357)
XLA Ops:
  4.9 49.3 %project.2 = (bf16[1536,2048]{1,0:T(8,128)(2,1)}, bf16[1536,2048]{1,0:T(8,128)(2,1)}, bf16[1536,2048]{1,0:T(8,128)(2,1)}) custom-call(bf16[1536,2048]{1,0:T(8,128)(2,1)} %bitcast.127, f32[1,2048]{1,0:T(1,128)} %get-tuple-element.23.gain_ref, bf16[2,2048,2048]{2,1,0:T(8,128)(2,1)} %query_w.3, bf16[2,2048,2048]{2,1,0:T(8,128)(2,1)} %key_w.3, ...), custom_call_target="tpu_custom_call" | custom-call | flops 38654705664 | bytes 50331648 | tf_op jit(solution)/shard_map/project/pallas_call | solution.py:83
  54.2 29.1 %attn_core.2 = bf16[1536,2048]{1,0:T(8,128)(2,1)} custom-call(bf16[1536,2048]{1,0:T(8,128)(2,1)} %get-tuple-element.11.q_ref, bf16[1536,2048]{1,0:T(8,128)(2,1)} %get-tuple-element.12.k_ref, bf16[1536,2048]{1,0:T(8,128)(2,1)} %get-tuple-element.13.v_ref, f32[16,512,512]{2,1,0:T(8,128)} %bias_ref.3, f32[3,1,512]{2,1,0:T(1,128)S(1)} %broadcast_in_dim.30.mask_ref), custom_call_target="tpu_custom_call" | custom-call | flops 6442450944 | bytes 41943040 | tf_op jit(solution)/shard_map/attn_core/pallas_call | solution.py:51
  83.3 19.6 %fusion = (f32[1536]{0:T(1024)S(1)}, bf16[1536,2048]{1,0:T(8,128)(2,1)}) fusion(bf16[1536,2048]{1,0:T(8,128)(2,1)} %attn_core.2, bf16[2,2048,2048]{2,1,0:T(8,128)(2,1)} %param.20, bf16[1536,2048]{1,0:T(8,128)(2,1)S(1)} %bitcast.128), kind=kOutput, calls=%fused_computation.6 | convolution fusion | flops 12903774208 | bytes 27269120 | tf_op jit(solution)/shard_map/dot_general | solution.py:99
  103.5 14.3 %fusion.27 = bf16[1536,2048]{1,0:T(8,128)(2,1)} fusion(s32[1536]{0:T(1024)S(1)} %get-tuple-element.20, bf16[1536,2048]{1,0:T(8,128)(2,1)} %get-tuple-element.28, f32[2048]{0:T(1024)S(1)} %bitcast.124, f32[1536]{0:T(1024)S(1)} %add_rsqrt_fusion.1), kind=kOutput, calls=%fused_computation.37 | convolution fusion | flops 9681764352 | bytes 12603392 | tf_op jit(solution)/shard_map/dot_general | solution.py:143
  117.9 8.8 all-to-all-start
  126.7 14.3 %fusion.29 = bf16[1536,2048]{1,0:T(8,128)(2,1)} fusion(s32[1536]{0:T(1024)S(1)} %get-tuple-element.18, bf16[1536,2048]{1,0:T(8,128)(2,1)} %get-tuple-element.28, f32[2048]{0:T(1024)S(1)} %bitcast.125, f32[1536]{0:T(1024)S(1)} %add_rsqrt_fusion.1), kind=kOutput, calls=%fused_computation.39 | convolution fusion | flops 9681764352 | bytes 12603392 | tf_op jit(solution)/shard_map/dot_general | solution.py:143
  141.0 70.3 %all-to-all-done = bf16[32,48,2048]{2,1,0:T(8,128)(2,1)} async-done(((bf16[32,48,2048]{2,1,0:T(8,128)(2,1)}), bf16[32,48,2048]{2,1,0:T(8,128)(2,1)}, u32[]{:S(2)}, u32[]{:S(2)}) %all-to-all-start) | async-done | bytes 6291488 | tf_op jit(solution)/shard_map/all_to_all | solution.py:144
  215.1 19.3 %convolution_convert_fusion.3 = bf16[1536,2048]{1,0:T(8,128)(2,1)} fusion(bf16[1536,2048]{1,0:T(8,128)(2,1)} %bitcast.10, bf16[2,2,1024,2048]{3,2,1,0:T(8,128)(2,1)} %param.23, bf16[2,2,2048,1024]{3,2,1,0:T(8,128)(2,1)} %param.22), kind=kOutput, calls=%fused_computation.46 | convolution fusion | flops 12891193344 | bytes 20971520 | tf_op jit(solution)/shard_map/dot_general | solution.py:147
  234.5 64.5 %all-to-all-done.2 = bf16[32,48,2048]{2,1,0:T(8,128)(2,1)} async-done(((bf16[32,48,2048]{2,1,0:T(8,128)(2,1)}), bf16[32,48,2048]{2,1,0:T(8,128)(2,1)}, u32[]{:S(2)}, u32[]{:S(2)}) %all-to-all-start.2) | async-done | bytes 6291488 | tf_op jit(solution)/shard_map/all_to_all | solution.py:144
  302.9 19.4 %convolution_convert_fusion.2 = bf16[1536,2048]{1,0:T(8,128)(2,1)} fusion(bf16[1536,2048]{1,0:T(8,128)(2,1)} %bitcast.16, bf16[2,2,1024,2048]{3,2,1,0:T(8,128)(2,1)} %param.23, bf16[2,2,2048,1024]{3,2,1,0:T(8,128)(2,1)} %param.22), kind=kOutput, calls=%fused_computation.45 | convolution fusion | flops 12891193344 | bytes 20971520 | tf_op jit(solution)/shard_map/dot_general | solution.py:147
  322.2 64.5 %all-to-all-done.1 = bf16[32,48,2048]{2,1,0:T(8,128)(2,1)} async-done(((bf16[32,48,2048]{2,1,0:T(8,128)(2,1)}), bf16[32,48,2048]{2,1,0:T(8,128)(2,1)}, u32[]{:S(2)}, u32[]{:S(2)}) %all-to-all-start.1) | async-done | bytes 6291488 | tf_op jit(solution)/shard_map/all_to_all | solution.py:148
  386.7 4.7 all-to-all-start.3
  391.5 15.1 %fusion.105 = (f32[1536]{0:T(1024)S(1)}, f32[1536,64]{0,1:T(8,128)S(1)}) fusion(f32[2,2048,64]{1,2,0:T(8,128)S(1)} %copy-done.9, bf16[1536,2048]{1,0:T(8,128)(2,1)} %get-tuple-element.28, f32[2048]{0:T(1024)S(1)} %bitcast.126, f32[1536]{0:T(1024)S(1)} %add_rsqrt_fusion.1), kind=kOutput, calls=%fused_computation.125 | convolution fusion | flops 2425453056 | bytes 7231488 | tf_op jit(solution)/shard_map/dot_general | solution.py:114
  407.4 14.0 %fusion.28 = bf16[1536,2048]{1,0:T(8,128)(2,1)} fusion(bf16[1536,2048]{1,0:T(8,128)(2,1)} %bitcast.14, s32[1536]{0:T(1024)S(1)} %get-tuple-element.20), kind=kOutput, calls=%fused_computation.38 | convolution fusion | flops 9669181440 | bytes 12589056 | tf_op jit(solution)/shard_map/dot_general | solution.py:149
  421.4 54.7 %all-to-all-done.3 = bf16[32,48,2048]{2,1,0:T(8,128)(2,1)} async-done(((bf16[32,48,2048]{2,1,0:T(8,128)(2,1)}), bf16[32,48,2048]{2,1,0:T(8,128)(2,1)}, u32[]{:S(2)}, u32[]{:S(2)}) %all-to-all-start.3) | async-done | bytes 6291488 | tf_op jit(solution)/shard_map/all_to_all | solution.py:148
  476.1 17.7 %fusion.5.hid_ref = bf16[1536,2048]{1,0:T(8,128)(2,1)} fusion(bf16[1536,2048]{1,0:T(8,128)(2,1)} %get-tuple-element.28, bf16[1536,2048]{1,0:T(8,128)(2,1)} %fusion.28, bf16[1536,2048]{1,0:T(8,128)(2,1)} %bitcast.20, f32[1536]{0:T(1024)S(1)} %select_reduce_fusion.1, s32[1536]{0:T(1024)S(1)} %get-tuple-element.18), kind=kOutput, calls=%fused_computation.10 | convolution fusion | flops 9684910080 | bytes 25178112 | tf_op jit(solution)/shard_map/dot_general | solution.py:149
  493.7 49.2 %project.3 = (bf16[1536,2048]{1,0:T(8,128)(2,1)}, bf16[1536,2048]{1,0:T(8,128)(2,1)}, bf16[1536,2048]{1,0:T(8,128)(2,1)}) custom-call(bf16[1536,2048]{1,0:T(8,128)(2,1)} %fusion.5.hid_ref, f32[1,2048]{1,0:T(1,128)} %get-tuple-element.24.gain_ref, bf16[2,2048,2048]{2,1,0:T(8,128)(2,1)} %query_w.3, bf16[2,2048,2048]{2,1,0:T(8,128)(2,1)} %key_w.3, ...), custom_call_target="tpu_custom_call" | custom-call | flops 38654705664 | bytes 50331648 | tf_op jit(solution)/shard_map/project/pallas_call | solution.py:83
  543.0 29.4 %attn_core.3 = bf16[1536,2048]{1,0:T(8,128)(2,1)} custom-call(bf16[1536,2048]{1,0:T(8,128)(2,1)} %get-tuple-element.14.q_ref, bf16[1536,2048]{1,0:T(8,128)(2,1)} %get-tuple-element.15.k_ref, bf16[1536,2048]{1,0:T(8,128)(2,1)} %get-tuple-element.16.v_ref, f32[16,512,512]{2,1,0:T(8,128)} %bias_ref.3, f32[3,1,512]{2,1,0:T(1,128)S(1)} %copy-done.1), custom_call_target="tpu_custom_call" | custom-call | flops 6442450944 | bytes 41943040 | tf_op jit(solution)/shard_map/attn_core/pallas_call | solution.py:51
  572.4 18.7 %fusion.6 = (f32[1536]{0:T(1024)S(1)}, bf16[1536,2048]{1,0:T(8,128)(2,1)S(1)}) fusion(bf16[1536,2048]{1,0:T(8,128)(2,1)} %attn_core.3, bf16[2,2048,2048]{2,1,0:T(8,128)(2,1)} %param.20, bf16[1536,2048]{1,0:T(8,128)(2,1)} %fusion.5.hid_ref), kind=kOutput, calls=%fused_computation.11 | convolution fusion | flops 12903774208 | bytes 27269120 | tf_op jit(solution)/shard_map/dot_general | solution.py:99
  591.1 12.7 %fusion.30 = bf16[1536,2048]{1,0:T(8,128)(2,1)} fusion(s32[1536]{0:T(1024)S(1)} %copy-done.6, bf16[1536,2048]{1,0:T(8,128)(2,1)S(1)} %get-tuple-element.32, f32[2048]{0:T(1024)S(1)} %bitcast.121, f32[1536]{0:T(1024)S(1)} %add_rsqrt_fusion), kind=kOutput, calls=%fused_computation.40 | convolution fusion | flops 9681764352 | bytes 12603392 | tf_op jit(solution)/shard_map/dot_general | solution.py:143
  603.8 4.1 all-to-all-start.4
  608.0 14.3 %fusion.32 = bf16[1536,2048]{1,0:T(8,128)(2,1)} fusion(s32[1536]{0:T(1024)S(1)} %copy-done.5, bf16[1536,2048]{1,0:T(8,128)(2,1)} %copy-done.11, f32[2048]{0:T(1024)S(1)} %bitcast.122, f32[1536]{0:T(1024)S(1)} %add_rsqrt_fusion), kind=kOutput, calls=%fused_computation.42 | convolution fusion | flops 9681764352 | bytes 12603392 | tf_op jit(solution)/shard_map/dot_general | solution.py:143
  622.3 70.0 %all-to-all-done.4 = bf16[32,48,2048]{2,1,0:T(8,128)(2,1)} async-done(((bf16[32,48,2048]{2,1,0:T(8,128)(2,1)}), bf16[32,48,2048]{2,1,0:T(8,128)(2,1)}, u32[]{:S(2)}, u32[]{:S(2)}) %all-to-all-start.4) | async-done | bytes 6291488 | tf_op jit(solution)/shard_map/all_to_all | solution.py:144
  696.1 19.3 %convolution_convert_fusion.1 = bf16[1536,2048]{1,0:T(8,128)(2,1)} fusion(bf16[1536,2048]{1,0:T(8,128)(2,1)} %bitcast.27, bf16[2,2,1024,2048]{3,2,1,0:T(8,128)(2,1)} %param.23, bf16[2,2,2048,1024]{3,2,1,0:T(8,128)(2,1)} %param.22), kind=kOutput, calls=%fused_computation.44 | convolution fusion | flops 12891193344 | bytes 20971520 | tf_op jit(solution)/shard_map/dot_general | solution.py:147
  715.5 64.5 %all-to-all-done.6 = bf16[32,48,2048]{2,1,0:T(8,128)(2,1)} async-done(((bf16[32,48,2048]{2,1,0:T(8,128)(2,1)}), bf16[32,48,2048]{2,1,0:T(8,128)(2,1)}, u32[]{:S(2)}, u32[]{:S(2)}) %all-to-all-start.6) | async-done | bytes 6291488 | tf_op jit(solution)/shard_map/all_to_all | solution.py:144
  783.9 19.3 %convolution_convert_fusion = bf16[1536,2048]{1,0:T(8,128)(2,1)} fusion(bf16[1536,2048]{1,0:T(8,128)(2,1)} %bitcast.33, bf16[2,2,1024,2048]{3,2,1,0:T(8,128)(2,1)} %param.23, bf16[2,2,2048,1024]{3,2,1,0:T(8,128)(2,1)} %param.22), kind=kOutput, calls=%fused_computation.43 | convolution fusion | flops 12891193344 | bytes 20971520 | tf_op jit(solution)/shard_map/dot_general | solution.py:147
  803.2 64.6 %all-to-all-done.5 = bf16[32,48,2048]{2,1,0:T(8,128)(2,1)} async-done(((bf16[32,48,2048]{2,1,0:T(8,128)(2,1)}), bf16[32,48,2048]{2,1,0:T(8,128)(2,1)}, u32[]{:S(2)}, u32[]{:S(2)}) %all-to-all-start.5) | async-done | bytes 6291488 | tf_op jit(solution)/shard_map/all_to_all | solution.py:148
  867.7 4.8 all-to-all-start.7
  872.5 15.1 %fusion.106 = (f32[1536]{0:T(1024)S(1)}, f32[1536,64]{0,1:T(8,128)S(1)}) fusion(f32[2,2048,64]{1,2,0:T(8,128)S(1)} %copy-done.10, bf16[1536,2048]{1,0:T(8,128)(2,1)} %copy-done.11, f32[2048]{0:T(1024)S(1)} %bitcast.123, f32[1536]{0:T(1024)S(1)} %add_rsqrt_fusion), kind=kOutput, calls=%fused_computation.126 | convolution fusion | flops 2425453056 | bytes 7231488 | tf_op jit(solution)/shard_map/dot_general | solution.py:114
  887.8 14.0 %fusion.31 = bf16[1536,2048]{1,0:T(8,128)(2,1)} fusion(bf16[1536,2048]{1,0:T(8,128)(2,1)} %bitcast.31, s32[1536]{0:T(1024)S(1)} %copy-done.6), kind=kOutput, calls=%fused_computation.41 | convolution fusion | flops 9669181440 | bytes 12589056 | tf_op jit(solution)/shard_map/dot_general | solution.py:149
  901.8 55.3 %all-to-all-done.7 = bf16[32,48,2048]{2,1,0:T(8,128)(2,1)} async-done(((bf16[32,48,2048]{2,1,0:T(8,128)(2,1)}), bf16[32,48,2048]{2,1,0:T(8,128)(2,1)}, u32[]{:S(2)}, u32[]{:S(2)}) %all-to-all-start.7) | async-done | bytes 6291488 | tf_op jit(solution)/shard_map/all_to_all | solution.py:148
  957.1 17.7 %fusion.11 = bf16[1536,2048]{1,0:T(8,128)(2,1)} fusion(bf16[1536,2048]{1,0:T(8,128)(2,1)} %copy-done.11, bf16[1536,2048]{1,0:T(8,128)(2,1)} %fusion.31, bf16[1536,2048]{1,0:T(8,128)(2,1)} %bitcast.37, f32[1536]{0:T(1024)S(1)} %select_reduce_fusion, s32[1536]{0:T(1024)S(1)} %copy-done.5), kind=kOutput, calls=%fused_computation.15 | convolution fusion | flops 9684910080 | bytes 25178112 | tf_op jit(solution)/shard_map/dot_general | solution.py:149
  (41 shorter events, 21.9 us)
Async XLA Ops:
  0.7 53.5 %copy-start = (f32[3,1,512]{2,1,0:T(1,128)}, f32[3,1,512]{2,1,0:T(1,128)S(1)}, u32[]{:S(2)}) copy-start(f32[3,1,512]{2,1,0:T(1,128)S(1)} %broadcast_in_dim.30.mask_ref) | copy-start | bytes 18436
  54.2 29.1 %copy-start.8 = (bf16[3,512,2048]{2,1,0:T(8,128)(2,1)S(1)}, bf16[3,512,2048]{2,1,0:T(8,128)(2,1)}, u32[]{:S(2)}) copy-start(bf16[3,512,2048]{2,1,0:T(8,128)(2,1)} %param.12) | copy-start | bytes 18874372
  117.9 93.4 %all-to-all-start = ((bf16[32,48,2048]{2,1,0:T(8,128)(2,1)}), bf16[32,48,2048]{2,1,0:T(8,128)(2,1)}, u32[]{:S(2)}, u32[]{:S(2)}) async-start(bf16[32,48,2048]{2,1,0:T(8,128)(2,1)} %bitcast.117), calls=%async_computation | async-start | bytes 12582912 | tf_op jit(solution)/shard_map/all_to_all | solution.py:144
  211.3 87.7 %all-to-all-start.2 = ((bf16[32,48,2048]{2,1,0:T(8,128)(2,1)}), bf16[32,48,2048]{2,1,0:T(8,128)(2,1)}, u32[]{:S(2)}, u32[]{:S(2)}) async-start(bf16[32,48,2048]{2,1,0:T(8,128)(2,1)} %bitcast.114), calls=%async_computation.2 | async-start | bytes 12582912 | tf_op jit(solution)/shard_map/all_to_all | solution.py:144
  299.0 87.7 %all-to-all-start.1 = ((bf16[32,48,2048]{2,1,0:T(8,128)(2,1)}), bf16[32,48,2048]{2,1,0:T(8,128)(2,1)}, u32[]{:S(2)}, u32[]{:S(2)}) async-start(bf16[32,48,2048]{2,1,0:T(8,128)(2,1)} %bitcast.112), calls=%async_computation.1 | async-start | bytes 12582912 | tf_op jit(solution)/shard_map/all_to_all | solution.py:148
  386.7 4.7 copy-start.9
  386.7 89.3 %all-to-all-start.3 = ((bf16[32,48,2048]{2,1,0:T(8,128)(2,1)}), bf16[32,48,2048]{2,1,0:T(8,128)(2,1)}, u32[]{:S(2)}, u32[]{:S(2)}) async-start(bf16[32,48,2048]{2,1,0:T(8,128)(2,1)} %bitcast.110), calls=%async_computation.3 | async-start | bytes 12582912 | tf_op jit(solution)/shard_map/all_to_all | solution.py:148
  391.5 15.2 %copy-start.4 = (s32[2,3,512]{2,0,1:T(2,128)S(1)}, s32[2,3,512]{2,0,1:T(2,128)}, u32[]{:S(2)}) copy-start(s32[2,3,512]{2,0,1:T(2,128)} %param.15) | copy-start | bytes 36868
  406.8 0.7 copy-start.2
  493.7 49.2 %copy-start.1 = (f32[3,1,512]{2,1,0:T(1,128)S(1)}, f32[3,1,512]{2,1,0:T(1,128)}, u32[]{:S(2)}) copy-start(f32[3,1,512]{2,1,0:T(1,128)} %copy-done) | copy-start | bytes 18436
  572.4 18.7 %copy-start.6 = (s32[1536]{0:T(1024)S(1)}, s32[1536]{0:T(1024)}, u32[]{:S(2)}) copy-start(s32[1536]{0:T(1024)} %get-tuple-element.19) | copy-start | bytes 18436
  572.4 18.8 %copy-start.7 = (f32[1,1,2048]{2,1,0:T(1,128)S(1)}, f32[1,1,2048]{2,1,0:T(1,128)}, u32[]{:S(2)}) copy-start(f32[1,1,2048]{2,1,0:T(1,128)} %get-tuple-element.21) | copy-start | bytes 24580
  591.1 12.7 %copy-start.11 = (bf16[1536,2048]{1,0:T(8,128)(2,1)}, bf16[1536,2048]{1,0:T(8,128)(2,1)S(1)}, u32[]{:S(2)}) copy-start(bf16[1536,2048]{1,0:T(8,128)(2,1)S(1)} %get-tuple-element.32) | copy-start | bytes 18874372
  603.8 4.1 copy-start.5
  603.8 88.5 %all-to-all-start.4 = ((bf16[32,48,2048]{2,1,0:T(8,128)(2,1)}), bf16[32,48,2048]{2,1,0:T(8,128)(2,1)}, u32[]{:S(2)}, u32[]{:S(2)}) async-start(bf16[32,48,2048]{2,1,0:T(8,128)(2,1)} %bitcast.116), calls=%async_computation.4 | async-start | bytes 12582912 | tf_op jit(solution)/shard_map/all_to_all | solution.py:144
  692.3 87.7 %all-to-all-start.6 = ((bf16[32,48,2048]{2,1,0:T(8,128)(2,1)}), bf16[32,48,2048]{2,1,0:T(8,128)(2,1)}, u32[]{:S(2)}, u32[]{:S(2)}) async-start(bf16[32,48,2048]{2,1,0:T(8,128)(2,1)} %bitcast.115), calls=%async_computation.6 | async-start | bytes 12582912 | tf_op jit(solution)/shard_map/all_to_all | solution.py:144
  780.0 87.7 %all-to-all-start.5 = ((bf16[32,48,2048]{2,1,0:T(8,128)(2,1)}), bf16[32,48,2048]{2,1,0:T(8,128)(2,1)}, u32[]{:S(2)}, u32[]{:S(2)}) async-start(bf16[32,48,2048]{2,1,0:T(8,128)(2,1)} %bitcast.113), calls=%async_computation.5 | async-start | bytes 12582912 | tf_op jit(solution)/shard_map/all_to_all | solution.py:148
  867.7 4.8 copy-start.10
  867.7 89.4 %all-to-all-start.7 = ((bf16[32,48,2048]{2,1,0:T(8,128)(2,1)}), bf16[32,48,2048]{2,1,0:T(8,128)(2,1)}, u32[]{:S(2)}, u32[]{:S(2)}) async-start(bf16[32,48,2048]{2,1,0:T(8,128)(2,1)} %bitcast.111), calls=%async_computation.7 | async-start | bytes 12582912 | tf_op jit(solution)/shard_map/all_to_all | solution.py:148
  872.5 15.2 %copy-start.3 = (pred[2,1536,64]{1,2,0:T(8,128)(4,1)S(1)}, pred[2,1536,64]{1,2,0:T(8,128)(4,1)}, u32[]{:S(2)}) copy-start(pred[2,1536,64]{1,2,0:T(8,128)(4,1)} %copy-done.2) | copy-start | bytes 589828
